TPU v7x, 32 devices: a whole 2x2x4 slice. The times are simulated.
32 devices in a mesh: seq: 8 (over z, x), head: 4 (over y, core).
Axes of the slice: x: 2, y: 2, z: 4, core: 2. Of those that a mesh axis runs over, the one named last changes fastest.
Arguments:
- states: bfloat16 [4096, 2048], P('seq'), may hold values from -6 to 6
- inner_weight: bfloat16 [2048, 4096], P(None, 'head'), may hold values from -0.125 to 0.125
- gate_weight: bfloat16 [2048, 4096], P(None, 'head'), may hold values from -1 to 1
- state_weight: bfloat16 [2048, 256], replicated, may hold values from -0.125 to 0.125
- step_weight: bfloat16 [2048, 32], P(None, 'head'), may hold values from -0.125 to 0.125
- step_bias: float32 [32], P('head'), may hold values from -4 to -2
- decay_rate: float32 [32], P('head'), may hold values from 0 to 1
- skip_gain: float32 [32], P('head'), may hold values from 0.5 to 1.5
- conv_inner: float32 [4, 4096], P(None, 'head'), may hold values from -3 to 3
- conv_state: float32 [4, 256], replicated, may hold values from -3 to 3
- norm_gain: float32 [4096], P('head'), may hold values from 0.5 to 2
- value_weight: float32 [4096], P('head'), may hold values from -0.09375 to 0.09375
- rewards: float32 [4096], P('seq'), may hold values from -4 to 4
- done_flags: int32 [4096], P('seq'), may hold values from 0 to 1, as said below
- horizon: int32 [4096], P('seq'), may hold values from 1 to 8
Outputs:
- values: float32 [4096], P('seq')
- targets: float32 [4096], P('seq')
- value_loss: float32 [], replicated
Inputs may be any that keep to these rules, and one draw needn't show every extreme that they name: `done_flags`: exactly one time step of the trajectory has an episode end.
All inputs are finite; a program needn't handle non-finite values.
Results may differ from a plain program's by a relative error of at most 0.007.
Values may be sent and summed in bfloat16 or wider, within the bound.
No kernel may reach another device: no remote copies, remote signals or barrier semaphores. Data moves between devices by JAX's collectives and lax.ppermute only.
A program may use at most 128 MiB of HBM per device.

v0:
```python
import math

import jax
import jax.numpy as jnp
from jax import lax
from jax.sharding import PartitionSpec as P

D_INNER = 4096
KCONV = 4
NSTEP = 8


DISCOUNT = 0.99
EXPECTILE = 0.7
EPSILON = 1e-05


def from_behind(block, axis, distance):
    devices = range(lax.axis_size(axis))
    route = [(i - distance, i) for i in devices if i - distance in devices]
    return lax.ppermute(block, axis, route)


def causal_conv(rim_rows, projected, kernel):
    padded = jnp.concatenate([rim_rows.astype(jnp.float32), projected.astype(jnp.float32)], axis=0)
    length = projected.shape[0]
    summed = jnp.zeros(projected.shape, jnp.float32)
    for offset in range(kernel.shape[0]):
        summed = summed + kernel[offset] * padded[offset : offset + length]
    return jax.nn.silu(summed).astype(jnp.bfloat16)


def block_scan(inner, writes, readout, step_size, decay_rate, done_int, running_state):
    precise = lax.Precision.HIGHEST
    inputs = step_size[:, :, None] * inner.astype(jnp.float32)
    local_decay = jnp.cumsum(-decay_rate * step_size, axis=0)
    done_count = jnp.cumsum(done_int)
    done_before = done_count - done_int
    scores = jnp.dot(readout, writes.T, preferred_element_type=jnp.float32)
    positions = jnp.arange(inner.shape[0])
    causal_mask = (positions[:, None] >= positions[None, :]) & (
        done_before[:, None] == done_before[None, :]
    )
    decay_gap = local_decay[:, None, :] - local_decay[None, :, :]
    weights = scores[:, :, None] * jnp.exp(jnp.where(causal_mask[:, :, None], decay_gap, -jnp.inf))
    block_out = jnp.einsum("tsh,shp->thp", weights, inputs, precision=precise)
    carry_reach = jnp.exp(local_decay) * (done_before == 0)[:, None]
    readout_float = readout.astype(jnp.float32)
    block_out = block_out + carry_reach[:, :, None] * jnp.einsum(
        "tn,hpn->thp", readout_float, running_state, precision=precise
    )
    tail_weight = (
        jnp.exp(local_decay[-1][None, :] - local_decay)
        * (done_count[-1] - done_before == 0)[:, None]
    )
    block_state = jnp.einsum(
        "shp,sn->hpn",
        tail_weight[:, :, None] * inputs,
        writes.astype(jnp.float32),
        precision=precise,
    )
    block_decay = jnp.exp(local_decay[-1]) * (done_count[-1] == 0)
    return (block_out, block_decay[:, None, None] * running_state + block_state, block_decay)


def nstep_targets(reward_ext, alive_ext, value_ext, horizon, length):
    targets = jnp.zeros((length,), jnp.float32)
    survive = jnp.ones((length,), jnp.float32)
    for offset in range(NSTEP + 1):
        factor = DISCOUNT**offset * survive
        targets = targets + jnp.where(
            offset < horizon, factor * reward_ext[offset : offset + length], 0.0
        )
        targets = targets + jnp.where(
            offset == horizon, factor * value_ext[offset : offset + length], 0.0
        )
        survive = survive * alive_ext[offset : offset + length]
    return targets


def expectile_terms(targets, values):
    residual = targets - values
    return jnp.where(residual < 0, 1.0 - EXPECTILE, EXPECTILE) * residual * residual


def per_device(
    states,
    inner_weight,
    gate_weight,
    state_weight,
    step_weight,
    step_bias,
    decay_rate,
    skip_gain,
    conv_inner,
    conv_state,
    norm_gain,
    value_weight,
    rewards,
    done_flags,
    horizon,
):
    token_count = states.shape[0]
    head_count = step_bias.shape[0]
    inner_width = inner_weight.shape[1]
    head_width = inner_width // head_count
    state_width = state_weight.shape[1] // 2
    inner_pre = jnp.dot(states, inner_weight, preferred_element_type=jnp.float32).astype(
        jnp.bfloat16
    )
    gate_pre = jnp.dot(states, gate_weight, preferred_element_type=jnp.float32).astype(jnp.bfloat16)
    state_pre = jnp.dot(states, state_weight, preferred_element_type=jnp.float32).astype(
        jnp.bfloat16
    )
    step_size = jax.nn.softplus(
        jnp.dot(states, step_weight, preferred_element_type=jnp.float32) + step_bias
    )
    conv_lag = KCONV - 1
    edge_rows = jnp.concatenate(
        [inner_pre[token_count - conv_lag :], state_pre[token_count - conv_lag :]], axis=1
    )
    rim_rows = from_behind(edge_rows, "seq", 1)
    inner_conv = causal_conv(rim_rows[:, :inner_width], inner_pre, conv_inner)
    state_conv = causal_conv(rim_rows[:, inner_width:], state_pre, conv_state)
    inner_heads = inner_conv.reshape(token_count, head_count, head_width)
    writes = state_conv[:, :state_width]
    readout = state_conv[:, state_width:]
    block_size = math.gcd(token_count, 256)
    running_state = jnp.zeros((head_count, head_width, state_width), jnp.float32)
    device_decay = jnp.ones((head_count,), jnp.float32)
    outputs = []
    for block_index in range(token_count // block_size):
        first_row = block_index * block_size
        last_row = first_row + block_size
        block_out, running_state, block_decay = block_scan(
            inner_heads[first_row:last_row],
            writes[first_row:last_row],
            readout[first_row:last_row],
            step_size[first_row:last_row],
            decay_rate,
            done_flags[first_row:last_row],
            running_state,
        )
        device_decay = device_decay * block_decay
        outputs.append(block_out)
    mixed_heads = jnp.concatenate(outputs, axis=0)
    everyone = lax.all_gather(device_decay[None, :], "seq", axis=0, tiled=True)
    seq_size = lax.axis_size("seq")
    seq_rank = lax.axis_index("seq")
    window_decay = jnp.concatenate([jnp.ones((1, head_count), jnp.float32), everyone[:-1]], axis=0)
    carried = from_behind(running_state, "seq", 1)
    stride = 1
    for round_index in range((seq_size - 1).bit_length()):
        partner = from_behind(carried, "seq", stride)
        own_window = lax.dynamic_index_in_dim(window_decay, seq_rank, 0, keepdims=False)
        carried = own_window[:, None, None] * partner + carried
        moved = jnp.concatenate(
            [jnp.ones((stride, head_count), jnp.float32), window_decay], axis=0
        )[:seq_size]
        window_decay = window_decay * moved
        stride = stride * 2
    full_decay = jnp.cumsum(-decay_rate * step_size, axis=0)
    full_before = jnp.cumsum(done_flags) - done_flags
    carry_reach = jnp.exp(full_decay) * (full_before == 0)[:, None]
    correction = jnp.einsum(
        "tn,hpn->thp", readout.astype(jnp.float32), carried, precision=lax.Precision.HIGHEST
    )
    mixed_heads = mixed_heads + carry_reach[:, :, None] * correction
    mixed_heads = mixed_heads + skip_gain[None, :, None] * inner_heads.astype(jnp.float32)
    gated = mixed_heads.reshape(token_count, inner_width) * jax.nn.silu(
        gate_pre.astype(jnp.float32)
    )
    square_part = jnp.sum(gated * gated, axis=1)
    square_sum = lax.psum(square_part, "head")
    normed = gated * lax.rsqrt(square_sum / D_INNER + EPSILON)[:, None] * norm_gain
    values = lax.psum(jnp.sum(normed * value_weight, axis=1), "head")
    alive = 1.0 - done_flags.astype(jnp.float32)
    leading = jnp.stack([rewards[:NSTEP], alive[:NSTEP], values[:NSTEP]], axis=0)
    following = from_behind(leading, "seq", -1)
    targets = nstep_targets(
        jnp.concatenate([rewards, following[0]]),
        jnp.concatenate([alive, following[1]]),
        jnp.concatenate([values, following[2]]),
        horizon,
        token_count,
    )
    local_loss = jnp.sum(expectile_terms(targets, values))
    value_loss = lax.psum(local_loss, "seq") / (token_count * lax.axis_size("seq"))
    return (values, targets, value_loss)


def solution(mesh):
    placed = (
        P("seq", None),
        P(None, "head"),
        P(None, "head"),
        P(),
        P(None, "head"),
        P("head"),
        P("head"),
        P("head"),
        P(None, "head"),
        P(),
        P("head"),
        P("head"),
        P("seq"),
        P("seq"),
        P("seq"),
    )
    return jax.shard_map(
        per_device, mesh=mesh, in_specs=placed, out_specs=(P("seq"), P("seq"), P()), check_vma=False
    )
```

profile of v0, /device:TPU:0, one launch (start us, length us, event | category | flops | bytes accessed | tf_op | source)
XLA Modules:
  0.0 174.0 jit_solution(13795237263150584330)
XLA Ops:
  0.7 1.6 copy-done
  2.2 5.9 %fusion.106 = (f32[512,1024]{1,0:T(8,128)}, bf16[512,1024]{1,0:T(8,128)(2,1)S(1)}) fusion(bf16[512,2048]{1,0:T(8,128)(2,1)S(1)} %copy-done, bf16[2048,1024]{1,0:T(8,128)(2,1)} %param.16), kind=kOutput, calls=%fused_computation.183 | convolution fusion | flops 2148532224 | bytes 9437184 | tf_op jit(solution)/shard_map/dot_general | solution.py:108
  8.1 1.5 fusion.107
  9.7 5.0 %collective-permute-start = (bf16[3,1280]{1,0:T(4,128)(2,1)S(1)}, bf16[3,1280]{1,0:T(4,128)(2,1)S(1)}, u32[]{:S(2)}, u32[]{:S(2)}) collective-permute-start(bf16[3,1280]{1,0:T(4,128)(2,1)S(1)} %pad_maximum_fusion.2), channel_id=1, source_target_pairs={{0,4},{4,8},{8,12},{12,16},{16,20},{20,24},{24,28},{1,5},{5,9},{9,... | collective-permute-start | bytes 23048 | tf_op jit(solution)/shard_map/ppermute | solution.py:21
  23.8 18.7 %all-gather = f32[8,1,8]{2,1,0:T(1,128)S(1)} all-gather(f32[1,1,8]{2,1,0:T(1,128)S(1)} %bitcast.142), channel_id=1, replica_groups=mesh['seq'=8,'head'=4] {'seq'}, dimensions={0}, use_global_device_ids=true | all-gather | bytes 288 | tf_op jit(solution)/shard_map/all_gather | solution.py:147
  48.1 4.7 %multiply_convert_fusion = bf16[512,1024]{1,0:T(8,128)(2,1)S(1)} fusion(f32[512,1024]{1,0:T(8,128)} %get-tuple-element.41, f32[3,1024]{1,0:T(4,128)S(1)} %slice_convert_fusion.2, f32[1024]{0:T(1024)S(1)} %bitcast.135, f32[1024]{0:T(1024)S(1)} %bitcast.136, f32[1024]{0:T(1024)S(1)} %bitcast.134, f32[1024]{0:T(1024)S(1)} %bitcast.133), kind=kLoop, calls=%fused_computation.31 | loop fusion | flops 7864320 | bytes 3174400 | tf_op jit(solution)/shard_map/convert_element_type | solution.py:30
  52.8 1.6 slice_convert_fusion
  54.4 2.5 %copy.53 = f32[256,1024]{0,1:T(8,128)} copy(f32[256,1024]{1,0:T(8,128)} %get-tuple-element.20) | data formatting | bytes 2097152 | tf_op jit(solution)/shard_map/convert_element_type | solution.py:35
  57.0 2.5 %copy.54 = f32[256,1024]{0,1:T(8,128)} copy(f32[256,1024]{1,0:T(8,128)} %get-tuple-element.19) | data formatting | bytes 2097152 | tf_op jit(solution)/shard_map/convert_element_type | solution.py:35
  59.5 2.1 %multiply_convert_fusion.1 = bf16[512,256]{1,0:T(8,128)(2,1)S(1)} fusion(f32[512,256]{1,0:T(8,128)} %get-tuple-element.45, f32[3,256]{1,0:T(4,128)S(1)} %slice_convert_fusion.3, f32[256]{0:T(256)} %bitcast.140, f32[256]{0:T(256)} %bitcast.141, f32[256]{0:T(256)} %bitcast.139, f32[256]{0:T(256)} %bitcast.138), kind=kLoop, calls=%fused_computation.81 | loop fusion | flops 1966080 | bytes 793600 | tf_op jit(solution)/shard_map/convert_element_type | solution.py:30
  61.6 1.9 %convolution_add_fusion.1 = f32[8,128,128]{2,1,0:T(8,128)S(1)} fusion(f32[256,8,128]{0,2,1:T(8,128)} %bitcast.128, f32[256,8]{0,1:T(8,128)} %get-tuple-element.50, f32[256,8]{0,1:T(8,128)S(1)} %get-tuple-element.24, f32[8]{0:T(128)} %get-tuple-element.52, bf16[512,256]{1,0:T(8,128)(2,1)S(1)} %multiply_convert_fusion.1), kind=kOutput, calls=%fused_computation.41 | convolution fusion | flops 403308544 | bytes 1654816 | tf_op jit(solution)/shard_map/shp,sn->hpn/dot_general | solution.py:56
  65.0 2.7 %collective-permute-start.1 = (f32[8,128,128]{2,1,0:T(8,128)S(1)}, f32[8,128,128]{2,1,0:T(8,128)}, u32[]{:S(2)}, u32[]{:S(2)}) collective-permute-start(f32[8,128,128]{2,1,0:T(8,128)S(1)} %convolution_add_fusion), channel_id=1, source_target_pairs={{0,4},{4,8},{8,12},{12,16},{16,20},{20,24},{24,28},{1,5},{5,9},{9,... | collective-permute-start | bytes 1572872 | tf_op jit(solution)/shard_map/ppermute | solution.py:21
  67.7 5.5 %convolution_convert_fusion = bf16[512,1024]{1,0:T(8,128)(2,1)} fusion(bf16[512,2048]{1,0:T(8,128)(2,1)S(1)} %copy-done, bf16[2048,1024]{1,0:T(8,128)(2,1)} %param.17), kind=kOutput, calls=%fused_computation.32 | convolution fusion | flops 2148007936 | bytes 7340032 | tf_op jit(solution)/shard_map/dot_general | solution.py:111
  74.2 5.3 %collective-permute-start.2 = (f32[8,128,128]{2,1,0:T(8,128)}, f32[8,128,128]{2,1,0:T(8,128)}, u32[]{:S(2)}, u32[]{:S(2)}) collective-permute-start(f32[8,128,128]{2,1,0:T(8,128)} %collective-permute-done.1), channel_id=1, source_target_pairs={{0,4},{4,8},{8,12},{12,16},{16,20},{20,24},{24,28},{1,5},{5,9},{9,... | collective-permute-start | bytes 1572872 | tf_op jit(solution)/shard_map/ppermute | solution.py:21
  80.2 1.6 copy.55
  82.5 1.6 convolution_multiply_fusion
  84.1 1.6 collective-permute-done.2
  85.7 1.3 multiply_add_fusion.1
  87.1 6.0 %collective-permute-start.3 = (f32[8,128,128]{2,1,0:T(8,128)S(1)}, f32[8,128,128]{2,1,0:T(8,128)S(1)}, u32[]{:S(2)}, u32[]{:S(2)}) collective-permute-start(f32[8,128,128]{2,1,0:T(8,128)S(1)} %multiply_add_fusion.1), channel_id=1, source_target_pairs={{0,8},{4,12},{8,16},{12,20},{16,24},{20,28},{1,9},{5,13},{9,17},{1... | collective-permute-start | bytes 1572872 | tf_op jit(solution)/shard_map/ppermute | solution.py:21
  93.3 2.7 %fusion.32 = f32[256,8,128]{0,2,1:T(8,128)S(1)} fusion(f32[256,8,128]{0,2,1:T(8,128)S(1)} %convolution_multiply_fusion, f32[256,8]{0,1:T(8,128)S(1)} %get-tuple-element.18, f32[256,256]{1,0:T(8,128)S(1)} %fusion.76, pred[256,256]{1,0:T(8,128)(4,1)S(1)} %copy-done.9, f32[256,8,128]{0,2,1:T(8,128)S(1)} %bitcast.131, f32[256,8]{0,1:T(8,128)S(1)} %get-tuple-element.23), kind=kOutput, calls=%fused_computation.37 | convolution fusion | flops 807403520 | bytes 3489792 | tf_op jit(solution)/shard_map/tsh,shp->thp/dot_general | solution.py:46
  95.9 6.9 %collective-permute-done.3 = f32[8,128,128]{2,1,0:T(8,128)S(1)} collective-permute-done((f32[8,128,128]{2,1,0:T(8,128)S(1)}, f32[8,128,128]{2,1,0:T(8,128)S(1)}, u32[]{:S(2)}, u32[]{:S(2)}) %collective-permute-start.3) | collective-permute-done | bytes 524320 | tf_op jit(solution)/shard_map/ppermute | solution.py:21
  103.0 9.0 %collective-permute-start.4 = (f32[8,128,128]{2,1,0:T(8,128)S(1)}, f32[8,128,128]{2,1,0:T(8,128)S(1)}, u32[]{:S(2)}, u32[]{:S(2)}) collective-permute-start(f32[8,128,128]{2,1,0:T(8,128)S(1)} %multiply_add_fusion), channel_id=1, source_target_pairs={{0,16},{4,20},{8,24},{12,28},{1,17},{5,21},{9,25},{13,29},{2,18},{... | collective-permute-start | bytes 1572872 | tf_op jit(solution)/shard_map/ppermute | solution.py:21
  112.2 2.7 %fusion.26 = f32[256,8,128]{0,2,1:T(8,128)S(1)} fusion(f32[256,8,128]{0,2,1:T(8,128)S(1)} %convolution_multiply_fusion.1, f32[256,8]{0,1:T(8,128)S(1)} %get-tuple-element.13, f32[256,256]{1,0:T(8,128)S(1)} %fusion.81, pred[256,256]{1,0:T(8,128)(4,1)S(1)} %get-tuple-element.48, f32[256,8,128]{0,2,1:T(8,128)S(1)} %bitcast.129, f32[256,8]{0,1:T(8,128)S(1)} %get-tuple-element.24), kind=kOutput, calls=%fused_computation.35 | convolution fusion | flops 807403520 | bytes 3489792 | tf_op jit(solution)/shard_map/tsh,shp->thp/dot_general | solution.py:46
  114.9 3.8 %collective-permute-done.4 = f32[8,128,128]{2,1,0:T(8,128)S(1)} collective-permute-done((f32[8,128,128]{2,1,0:T(8,128)S(1)}, f32[8,128,128]{2,1,0:T(8,128)S(1)}, u32[]{:S(2)}, u32[]{:S(2)}) %collective-permute-start.4) | collective-permute-done | bytes 524320 | tf_op jit(solution)/shard_map/ppermute | solution.py:21
  118.7 2.7 %fusion.12 = f32[512,8,128]{0,2,1:T(8,128)} fusion(f32[256,8,128]{0,2,1:T(8,128)S(1)} %fusion.32, f32[256,8,128]{0,2,1:T(8,128)S(1)} %fusion.26, f32[512,8,128]{0,2,1:T(8,128)S(1)} %bitcast.126, f32[8]{0:T(128)S(1)} %copy-done.25, f32[512,8]{0,1:T(8,128)S(1)} %fusion.87, f32[8,128,128]{2,1,0:T(8,128)S(1)} %multiply_add_fusion, ...), kind=kOutput, calls=%fused_computation.18 | convolution fusion | flops 808189952 | bytes 7488512 | tf_op jit(solution)/shard_map/tn,hpn->thp/dot_general | solution.py:165
  121.4 3.0 %copy.56 = f32[512,1024]{1,0:T(8,128)} copy(f32[512,1024]{0,1:T(8,128)} %bitcast.127) | data formatting | bytes 4194304 | tf_op jit(solution)/shard_map/reshape | solution.py:170
  124.4 3.6 %multiply_reduce_fusion.1 = (f32[512]{0:T(512)S(1)}, f32[512,1024]{1,0:T(8,128)}) fusion(f32[512,1024]{1,0:T(8,128)} %copy.56, bf16[512,1024]{1,0:T(8,128)(2,1)S(1)} %copy-done.6), kind=kLoop, calls=%fused_computation.20 | loop fusion | flops 4193792 | bytes 5244928 | tf_op jit(solution)/shard_map/reduce_sum | solution.py:173
  128.0 5.7 %psum.21 = f32[512]{0:T(512)S(1)} all-reduce(f32[512]{0:T(512)S(1)} %get-tuple-element.8), channel_id=1, replica_groups=mesh['seq'=8,'head'=4] {'head'}, use_global_device_ids=true, to_apply=%region_13.14 | all-reduce | flops 512 | bytes 4096 | tf_op jit(solution)/shard_map/psum | solution.py:174
  133.7 2.0 %multiply_reduce_fusion = f32[512]{0:T(512)S(1)} fusion(f32[512,1024]{1,0:T(8,128)} %get-tuple-element.9, f32[1024]{0:T(1024)S(1)} %copy-done.16, f32[1024]{0:T(1024)S(1)} %copy-done.17, f32[512]{0:T(512)S(1)} %add_rsqrt_fusion), kind=kLoop, calls=%fused_computation.19 | loop fusion | flops 2096640 | bytes 2109440 | tf_op jit(solution)/shard_map/reduce_sum | solution.py:176
  135.7 6.6 %psum.22 = f32[512]{0:T(512)S(1)} all-reduce(f32[512]{0:T(512)S(1)} %multiply_reduce_fusion), channel_id=1, replica_groups=mesh['seq'=8,'head'=4] {'head'}, use_global_device_ids=true, to_apply=%region_15.16 | all-reduce | flops 512 | bytes 4096 | tf_op jit(solution)/shard_map/psum | solution.py:176
  143.7 4.2 %collective-permute-done.5 = f32[3,8]{1,0:T(4,128)S(1)} collective-permute-done((f32[3,8]{1,0:T(4,128)S(1)}, f32[3,8]{1,0:T(4,128)S(1)}, u32[]{:S(2)}, u32[]{:S(2)}) %collective-permute-start.5) | collective-permute-done | bytes 128 | tf_op jit(solution)/shard_map/ppermute | solution.py:21
  149.2 23.0 %psum.23 = f32[]{:T(128)} all-reduce(f32[]{:T(128)} %get-tuple-element.6), channel_id=1, replica_groups=mesh['seq'=8,'head'=4] {'seq'}, use_global_device_ids=true, to_apply=%region_17.18 | all-reduce | flops 1 | bytes 8 | tf_op jit(solution)/shard_map/psum | solution.py:188
  (130 shorter events, 20.4 us)
Async XLA Ops:
  0.6 7.5 %copy-start.7 = (bf16[2048,256]{1,0:T(8,128)(2,1)S(1)}, bf16[2048,256]{1,0:T(8,128)(2,1)}, u32[]{:S(2)}) copy-start(bf16[2048,256]{1,0:T(8,128)(2,1)} %param.18) | copy-start | bytes 3145732
  8.1 6.6 %copy-start.8 = (s32[512]{0:T(512)S(1)}, s32[512]{0:T(512)}, u32[]{:S(2)}) copy-start(s32[512]{0:T(512)} %param.28) | copy-start | bytes 6148
  8.1 12.4 %copy-start.27 = (f32[8]{0:T(128)S(1)}, f32[8]{0:T(128)}, u32[]{:S(2)}) copy-start(f32[8]{0:T(128)} %param.21) | copy-start | bytes 100
  8.1 12.4 %copy-start.10 = (bf16[2048,8]{0,1:T(8,128)(2,1)S(1)}, bf16[2048,8]{0,1:T(8,128)(2,1)}, u32[]{:S(2)}) copy-start(bf16[2048,8]{0,1:T(8,128)(2,1)} %param.19) | copy-start | bytes 98308
  8.1 12.4 %copy-start.24 = (f32[8]{0:T(128)S(1)}, f32[8]{0:T(128)}, u32[]{:S(2)}) copy-start(f32[8]{0:T(128)} %param.20) | copy-start | bytes 100
  9.7 13.1 %copy-start.18 = (f32[4,256]{1,0:T(4,128)S(1)}, f32[4,256]{1,0:T(4,128)}, u32[]{:S(2)}) copy-start(f32[4,256]{1,0:T(4,128)} %param.24) | copy-start | bytes 12292
  9.7 13.7 %copy-start.12 = (f32[4,1024]{1,0:T(4,128)S(1)}, f32[4,1024]{1,0:T(4,128)}, u32[]{:S(2)}) copy-start(f32[4,1024]{1,0:T(4,128)} %param.23) | copy-start | bytes 49156
  9.7 37.3 %copy-start.13 = (f32[512]{0:T(512)S(1)}, f32[512]{0:T(512)}, u32[]{:S(2)}) copy-start(f32[512]{0:T(512)} %param.27) | copy-start | bytes 6148
  9.7 38.4 %collective-permute-start = (bf16[3,1280]{1,0:T(4,128)(2,1)S(1)}, bf16[3,1280]{1,0:T(4,128)(2,1)S(1)}, u32[]{:S(2)}, u32[]{:S(2)}) collective-permute-start(bf16[3,1280]{1,0:T(4,128)(2,1)S(1)} %pad_maximum_fusion.2), channel_id=1, source_target_pairs={{0,4},{4,8},{8,12},{12,16},{16,20},{20,24},{24,28},{1,5},{5,9},{9,... | collective-permute-start | bytes 23048 | tf_op jit(solution)/shard_map/ppermute | solution.py:21
  20.5 32.3 %copy-start.14 = (f32[512]{0:T(512)}, f32[512]{0:T(512)S(1)}, u32[]{:S(2)}) copy-start(f32[512]{0:T(512)S(1)} %convert_subtract_fusion) | copy-start | bytes 6148
  59.5 4.8 %copy-start.4 = (f32[256,1024]{0,1:T(8,128)S(1)}, f32[256,1024]{0,1:T(8,128)}, u32[]{:S(2)}) copy-start(f32[256,1024]{0,1:T(8,128)} %copy.54) | copy-start | bytes 3145732
  59.5 4.8 %copy-start.20 = (f32[8]{0:T(128)S(1)}, f32[8]{0:T(128)}, u32[]{:S(2)}) copy-start(f32[8]{0:T(128)} %get-tuple-element.51) | copy-start | bytes 100
  65.0 9.2 %collective-permute-start.1 = (f32[8,128,128]{2,1,0:T(8,128)S(1)}, f32[8,128,128]{2,1,0:T(8,128)}, u32[]{:S(2)}, u32[]{:S(2)}) collective-permute-start(f32[8,128,128]{2,1,0:T(8,128)S(1)} %convolution_add_fusion), channel_id=1, source_target_pairs={{0,4},{4,8},{8,12},{12,16},{16,20},{20,24},{24,28},{1,5},{5,9},{9,... | collective-permute-start | bytes 1572872 | tf_op jit(solution)/shard_map/ppermute | solution.py:21
  74.2 11.5 %collective-permute-start.2 = (f32[8,128,128]{2,1,0:T(8,128)}, f32[8,128,128]{2,1,0:T(8,128)}, u32[]{:S(2)}, u32[]{:S(2)}) collective-permute-start(f32[8,128,128]{2,1,0:T(8,128)} %collective-permute-done.1), channel_id=1, source_target_pairs={{0,4},{4,8},{8,12},{12,16},{16,20},{20,24},{24,28},{1,5},{5,9},{9,... | collective-permute-start | bytes 1572872 | tf_op jit(solution)/shard_map/ppermute | solution.py:21
  81.9 3.9 %copy-start.19 = (f32[8]{0:T(128)S(1)}, f32[8]{0:T(128)}, u32[]{:S(2)}) copy-start(f32[8]{0:T(128)} %fusion.99) | copy-start | bytes 100
  81.9 11.4 %copy-start.5 = (f32[256,1024]{0,1:T(8,128)S(1)}, f32[256,1024]{0,1:T(8,128)}, u32[]{:S(2)}) copy-start(f32[256,1024]{0,1:T(8,128)} %copy.54) | copy-start | bytes 3145732
  81.9 11.4 %copy-start.9 = (pred[256,256]{1,0:T(8,128)(4,1)S(1)}, pred[256,256]{1,0:T(8,128)(4,1)}, u32[]{:S(2)}) copy-start(pred[256,256]{1,0:T(8,128)(4,1)} %get-tuple-element.47) | copy-start | bytes 196612
  87.1 15.8 %copy-start.26 = (f32[8]{0:T(128)S(1)}, f32[8]{0:T(128)}, u32[]{:S(2)}) copy-start(f32[8]{0:T(128)} %fusion.98) | copy-start | bytes 100
  87.1 15.8 %collective-permute-start.3 = (f32[8,128,128]{2,1,0:T(8,128)S(1)}, f32[8,128,128]{2,1,0:T(8,128)S(1)}, u32[]{:S(2)}, u32[]{:S(2)}) collective-permute-start(f32[8,128,128]{2,1,0:T(8,128)S(1)} %multiply_add_fusion.1), channel_id=1, source_target_pairs={{0,8},{4,12},{8,16},{12,20},{16,24},{20,28},{1,9},{5,13},{9,17},{1... | collective-permute-start | bytes 1572872 | tf_op jit(solution)/shard_map/ppermute | solution.py:21
  93.2 19.0 %copy-start.3 = (f32[256,1024]{0,1:T(8,128)S(1)}, f32[256,1024]{0,1:T(8,128)}, u32[]{:S(2)}) copy-start(f32[256,1024]{0,1:T(8,128)} %copy.53) | copy-start | bytes 3145732
  103.0 15.8 %copy-start.1 = (f32[512,1024]{0,1:T(8,128)S(1)}, f32[512,1024]{0,1:T(8,128)}, u32[]{:S(2)}) copy-start(f32[512,1024]{0,1:T(8,128)} %copy.55) | copy-start | bytes 6291460
  103.0 15.8 %copy-start.25 = (f32[8]{0:T(128)S(1)}, f32[8]{0:T(128)}, u32[]{:S(2)}) copy-start(f32[8]{0:T(128)} %param.22) | copy-start | bytes 100
  103.0 15.7 %collective-permute-start.4 = (f32[8,128,128]{2,1,0:T(8,128)S(1)}, f32[8,128,128]{2,1,0:T(8,128)S(1)}, u32[]{:S(2)}, u32[]{:S(2)}) collective-permute-start(f32[8,128,128]{2,1,0:T(8,128)S(1)} %multiply_add_fusion), channel_id=1, source_target_pairs={{0,16},{4,20},{8,24},{12,28},{1,17},{5,21},{9,25},{13,29},{2,18},{... | collective-permute-start | bytes 1572872 | tf_op jit(solution)/shard_map/ppermute | solution.py:21
  121.4 3.0 %copy-start.6 = (bf16[512,1024]{1,0:T(8,128)(2,1)S(1)}, bf16[512,1024]{1,0:T(8,128)(2,1)}, u32[]{:S(2)}) copy-start(bf16[512,1024]{1,0:T(8,128)(2,1)} %convolution_convert_fusion) | copy-start | bytes 3145732
  124.4 9.3 %copy-start.16 = (f32[1024]{0:T(1024)S(1)}, f32[1024]{0:T(1024)}, u32[]{:S(2)}) copy-start(f32[1024]{0:T(1024)} %param.26) | copy-start | bytes 12292
  124.4 9.3 %copy-start.17 = (f32[1024]{0:T(1024)S(1)}, f32[1024]{0:T(1024)}, u32[]{:S(2)}) copy-start(f32[1024]{0:T(1024)} %param.25) | copy-start | bytes 12292
  128.0 14.4 %copy-start.22 = (f32[1,8]{1,0:T(1,128)S(1)}, f32[1,8]{1,0:T(1,128)}, u32[]{:S(2)}) copy-start(f32[1,8]{1,0:T(1,128)} %get-tuple-element.53) | copy-start | bytes 100
  128.0 14.4 %copy-start.23 = (f32[1,8]{1,0:T(1,128)S(1)}, f32[1,8]{1,0:T(1,128)}, u32[]{:S(2)}) copy-start(f32[1,8]{1,0:T(1,128)} %get-tuple-element.54) | copy-start | bytes 100
  128.0 19.9 %copy-start.15 = (f32[512]{0:T(512)S(1)}, f32[512]{0:T(512)}, u32[]{:S(2)}) copy-start(f32[512]{0:T(512)} %copy-done.14) | copy-start | bytes 6148
  128.0 19.9 %copy-start.21 = (s32[512]{0:T(512)S(1)}, s32[512]{0:T(512)}, u32[]{:S(2)}) copy-start(s32[512]{0:T(512)} %param.29) | copy-start | bytes 6148
  142.4 30.5 %copy-start.11 = (f32[512]{0:T(512)}, f32[512]{0:T(512)S(1)}, u32[]{:S(2)}) copy-start(f32[512]{0:T(512)S(1)} %psum.22) | copy-start | bytes 6148
  142.4 5.5 %collective-permute-start.5 = (f32[3,8]{1,0:T(4,128)S(1)}, f32[3,8]{1,0:T(4,128)S(1)}, u32[]{:S(2)}, u32[]{:S(2)}) collective-permute-start(f32[3,8]{1,0:T(4,128)S(1)} %pad_maximum_fusion.8), channel_id=1, source_target_pairs={{4,0},{8,4},{12,8},{16,12},{20,16},{24,20},{28,24},{5,1},{9,5},{13... | collective-permute-start | bytes 296 | tf_op jit(solution)/shard_map/ppermute | solution.py:21
  (2 other events, 2.4 us)
where the time goes:
time: 175 us; the launch traced here: 174 us
  blocking collectives  54 us (31%)
  starting transfers between devices  29.3 us (17%)
  matrix products  26.7 us (15%)
  other arithmetic  24.9 us (14%)
  waiting for transfers between devices  17.6 us (10%)
  local copies, waits for them, and re-layouts  17.5 us (10%)
  between operations  4.12 us (2%)
    ppermute x6, starting transfers between devices, from_behind(): return lax.ppermute(block, axis, route)  29.3 us
    psum x1, blocking collectives, per_device(): lax.psum(local_loss, 'seq') / (token_count * lax.axis_size('seq'))  23 us
    all_gather x1, blocking collectives, per_device(): everyone = lax.all_gather(device_decay[None, :], 'seq', axis=0, tiled=True)  18.7 us
    ppermute x6, waiting for transfers between devices, from_behind(): return lax.ppermute(block, axis, route)  17.6 us
    convert_element_type x2, other arithmetic, causal_conv(): return jax.nn.silu(summed).astype(jnp.bfloat16)  6.75 us
    psum x1, blocking collectives, per_device(): values = lax.psum(jnp.sum(normed * value_weight, axis=1), 'head')  6.64 us
    dot_general x1, matrix products, per_device(): jnp.dot(states, inner_weight, preferred_element_type=jnp.float32)  5.87 us
    psum x1, blocking collectives, per_device(): square_sum = lax.psum(square_part, 'head')  5.67 us
  transfers between devices with their start and end apart: 6, of which 5 were waited for; matrix products, arithmetic and copies ran while one was open for 17% of the time, Pallas kernels for 0%

commit v1 on v0

v1 whole, which is shorter than its diff:
```python
import functools

import jax
import jax.numpy as jnp
from jax import lax
from jax.experimental import pallas as pl
from jax.experimental.pallas import tpu as pltpu
from jax.sharding import PartitionSpec as P

D_INNER = 4096
NSTEP = 8
DISCOUNT = 0.99
EXPECTILE = 0.7
EPSILON = 1e-05
LANES = 128
HALO = 8
SERIES = 32
RESET = 300.0
VMEM = pl.BlockSpec(memory_space=pltpu.VMEM)
SMEM = pl.BlockSpec(memory_space=pltpu.SMEM)
ANY = pl.BlockSpec(memory_space=pl.ANY)
F32 = jnp.float32
BF16 = jnp.bfloat16


def call(body, outs, ins, scratch=(), flops=0, name=None):
    return pl.pallas_call(
        body,
        out_shape=outs,
        in_specs=ins,
        out_specs=jax.tree.map(lambda _: VMEM, outs),
        scratch_shapes=list(scratch),
        cost_estimate=pl.CostEstimate(flops=flops, transcendentals=0, bytes_accessed=0),
        compiler_params=pltpu.CompilerParams(vmem_limit_bytes=60 * 2**20),
        name=name,
    )


def dot(a, b, dims=((1,), (0,))):
    return lax.dot_general(a, b, (dims, ((), ())), preferred_element_type=F32)


def silu(x):
    return x * jax.nn.sigmoid(x)


def column(scalars, count, shape):
    row = lax.broadcasted_iota(jnp.int32, shape, 0)
    out = jnp.zeros(shape, F32)
    for h in range(count):
        out = jnp.where(row == h, scalars[h], out)
    return out


def project_body(
    bias, decay, done, states, inner_w, state_w, step_w, inner_pre, state_pre, rows, cols, raw
):
    length = states.shape[0]
    heads = bias.shape[0]
    raw[:, :heads] = dot(states[...], step_w[...])
    shape = (heads, length)
    step = raw[...].T[:heads] + column(bias, heads, shape)
    step = jnp.maximum(step, 0.0) + jnp.log1p(jnp.exp(-jnp.abs(step)))
    ended = jnp.broadcast_to(done[...].astype(F32) * RESET, shape)
    total = -column(decay, heads, shape) * step - ended
    lane = lax.broadcasted_iota(jnp.int32, shape, 1)
    stride = 1
    while stride < length:
        total = total + jnp.where(lane >= stride, pltpu.roll(total, stride, 1), 0.0)
        stride *= 2
    reach = total + ended
    last = total[:, length - 1 :]
    rows[0:heads] = reach
    rows[heads : 2 * heads] = step
    rows[2 * heads :] = jnp.broadcast_to(jnp.exp(last), shape)
    tail = jnp.exp(last - reach) * step
    fill = jnp.zeros((LANES - 3 * heads, length), F32)
    cols[...] = jnp.concatenate([tail, reach, jnp.exp(reach), fill], axis=0).T
    width = 256
    for c in range(0, state_w.shape[1], width):
        state_pre[:, c : c + width] = dot(states[...], state_w[:, c : c + width]).astype(BF16)
    for c in range(0, inner_w.shape[1], width):
        inner_pre[:, c : c + width] = dot(states[...], inner_w[:, c : c + width]).astype(BF16)


def conv_body(
    halo,
    inner_w,
    state_w,
    inner_pre,
    state_pre,
    taps_inner,
    taps_state,
    rows,
    cols,
    rewards,
    done,
    horizon,
    inner,
    state,
    message,
    pad,
    weighted,
):
    length = inner_pre.shape[0]
    heads = rows.shape[0] // 3
    shards, depth = message.shape[0], message.shape[1] - 2 * heads - SERIES
    block = LANES

    def convolve(rim, source, taps, target, c, scaled):
        slot = pad.at[c % 2]
        at = slice(c * LANES, (c + 1) * LANES)
        slot[0:HALO] = rim
        slot[HALO:] = source[:, at].astype(F32)
        for r in range(0, length, block):
            out = taps[0:1, at] * slot[r + HALO - 3 : r + HALO - 3 + block]
            for k in range(1, 4):
                out = out + taps[k : k + 1, at] * slot[r + HALO - 3 + k : r + HALO - 3 + k + block]
            out = silu(out).astype(BF16)
            target[r : r + block, at] = out
            if scaled:
                scale = cols[r : r + block, c : c + 1]
                weighted[r : r + block, at] = (out.astype(F32) * scale).astype(BF16)

    rim = dot(halo[...], state_w[...]).astype(BF16).astype(F32)
    for c in range(state_pre.shape[1] // LANES):
        convolve(rim[:, c * LANES : (c + 1) * LANES], state_pre, taps_state, state, c, False)
    writes = state[:, :LANES].astype(F32).T.astype(BF16)
    pair = 2 * LANES
    for c in range(0, heads, 2):
        at = slice(c * LANES, c * LANES + pair)
        rim = dot(halo[...], inner_w[:, at]).astype(BF16).astype(F32)
        convolve(rim[:, :LANES], inner_pre, taps_inner, inner, c, True)
        convolve(rim[:, LANES:], inner_pre, taps_inner, inner, c + 1, True)
        summary = dot(writes, weighted[:, at]).astype(BF16)
        for half in range(2):
            own = summary[:, half * LANES : (half + 1) * LANES]
            first = (c + half) * LANES
            step = min(depth, LANES)
            for q in range(0, LANES, step):
                dest, at_row = divmod(first + q, depth)
                message[dest, at_row : at_row + step] = own[q : q + step]
    total = rows[2 * heads :, 0:LANES]
    high = total.astype(BF16).astype(F32)
    per_row = length // LANES
    split = lambda ref: [ref[:, q * LANES : (q + 1) * LANES].astype(F32) for q in range(per_row)]
    reward = split(rewards)
    first = [r.astype(BF16).astype(F32) for r in reward]
    second = [(r - a).astype(BF16).astype(F32) for r, a in zip(reward, first)]
    third = [r - a - b for r, a, b in zip(reward, first, second)]
    stack = first + second + third + split(done) + split(horizon)
    stack.append(jnp.zeros((SERIES - len(stack), LANES), F32))
    extra = jnp.concatenate([high, total - high] + stack, axis=0).astype(BF16)
    for dest in range(shards):
        message[dest, depth:] = extra


def gate_body(states, gate_w, after, gate):
    del after
    width = 256
    for c in range(0, gate_w.shape[1], width):
        pre = dot(states[...], gate_w[:, c : c + width]).astype(BF16).astype(F32)
        gate[:, c : c + width] = silu(pre)


def scan_body(rank, received, carried):
    shards, depth = carried.shape[0], carried.shape[1]
    heads = shards * depth // LANES
    part = min(depth, LANES)
    row = lax.broadcasted_iota(jnp.int32, (2 * heads, LANES), 0)
    for q in range(0, depth, part):
        head = lax.div(rank[0] * depth + q, LANES)
        state = jnp.zeros((part, LANES), F32)
        for j in range(shards):
            carried[j, q : q + part] = state.astype(BF16)
            both = received[j, depth : depth + 2 * heads].astype(F32)
            keep = (row == head) | (row == head + heads)
            decay = jnp.sum(jnp.where(keep, both, 0.0), axis=0, keepdims=True)
            state = decay * state + received[j, q : q + part].astype(F32)


def shift_time(x, distance):
    lane = lax.broadcasted_iota(jnp.int32, x.shape, 1)
    row = lax.broadcasted_iota(jnp.int32, x.shape, 0)
    count = x.shape[0]
    below = jnp.where(row < count - 1, pltpu.roll(x, count - 1, 0), 0.0)
    moved = jnp.where(lane < distance, below, x)
    return pltpu.roll(moved, LANES - distance, 1)


def inside_body(
    skip, inner, state, rows, cols, received, local, returns, code, scores, reward_s, alive_s, steps_s
):
    length = inner.shape[0]
    heads = rows.shape[0] // 3
    block = LANES
    readout = state[:, LANES:]
    writes = state[:, :LANES]
    scores[...] = dot(readout, writes, ((1,), (1,)))
    below = lax.broadcasted_iota(jnp.int32, (block, block), 0) >= lax.broadcasted_iota(
        jnp.int32, (block, block), 1
    )
    for h in range(heads):
        at = slice(h * LANES, (h + 1) * LANES)
        for r in range(0, length, block):
            here = jnp.broadcast_to(cols[r : r + block, heads + h : heads + h + 1], (block, LANES))
            pieces = []
            for s in range(0, r + block, block):
                gap = here - rows[h : h + 1, s : s + block]
                if s == r:
                    gap = jnp.where(below, gap, -jnp.inf)
                weight = scores[r : r + block, s : s + block] * rows[heads + h : heads + h + 1, s : s + block]
                pieces.append((jnp.exp(gap) * weight).astype(BF16))
            weights = jnp.concatenate(pieces, axis=1)
            out = dot(weights, inner[0 : r + block, at])
            local[r : r + block, at] = out + skip[h] * inner[r : r + block, at].astype(F32)
    shards = received.shape[0]
    series = received.shape[1] - SERIES
    per = length // LANES
    for j in range(shards):
        extra = received[j, series:].astype(F32)
        to = slice(j * per, (j + 1) * per)
        reward_s[to] = extra[0:per] + extra[per : 2 * per] + extra[2 * per : 3 * per]
        alive_s[to] = 1.0 - extra[3 * per : 4 * per]
        steps_s[to] = extra[4 * per : 5 * per]
    reward, alive, steps = reward_s[...], alive_s[...], steps_s[...]
    gained = jnp.zeros(reward.shape, F32)
    survive = jnp.ones(reward.shape, F32)
    reached = jnp.zeros(reward.shape, F32)
    for offset in range(NSTEP + 1):
        ahead = shift_time(reward, offset) if offset else reward
        gained = gained + jnp.where(offset < steps, DISCOUNT**offset * survive * ahead, 0.0)
        reached = jnp.where(offset == steps, survive * offset, reached)
        if offset < NSTEP:
            survive = survive * (shift_time(alive, offset) if offset else alive)
    returns[...] = gained
    code[...] = reached


def finish_body(state, carried, local, gate, cols, norm_gain, value_weight, message):
    length = state.shape[0]
    heads = carried.shape[0] // LANES
    block = LANES
    weight = norm_gain[...] * value_weight[...]
    squares, sums = [], []
    for r in range(0, length, block):
        readout = state[r : r + block, LANES:]
        square = jnp.zeros((block, LANES), F32)
        total = jnp.zeros((block, LANES), F32)
        for c in range(0, heads, 2):
            both = jnp.concatenate(
                [carried[(c + i) * LANES : (c + i + 1) * LANES] for i in range(2)], axis=1
            )
            fix = dot(readout, both)
            for i in range(2):
                h = c + i
                at = slice(h * LANES, (h + 1) * LANES)
                reach = cols[r : r + block, 2 * heads + h : 2 * heads + h + 1]
                mixed = local[r : r + block, at] + reach * fix[:, i * LANES : (i + 1) * LANES]
                gated = mixed * gate[r : r + block, at]
                square = square + gated * gated
                total = total + gated * weight[:, at]
        squares.append(jnp.sum(square.T, axis=0, keepdims=True))
        sums.append(jnp.sum(total.T, axis=0, keepdims=True))
    tile = jnp.concatenate(squares + sums, axis=0)
    for dest in range(message.shape[0]):
        message[dest] = tile


def loss_body(rank, received, returns, code, values, targets, loss, values_s, targets_s):
    devices, double, _ = received.shape
    per = double // 2
    total_rows = returns.shape[0]
    shards = total_rows // per
    group = devices // shards
    for j in range(shards):
        tile = received[group * j]
        for g in range(1, group):
            tile = tile + received[group * j + g]
        values_s[per * j : per * (j + 1)] = tile[per:] * lax.rsqrt(tile[:per] / D_INNER + EPSILON)
    value = values_s[...]
    reached = code[...]
    target = returns[...]
    for offset in range(1, NSTEP + 1):
        ahead = shift_time(value, offset)
        target = target + jnp.where(reached == offset, DISCOUNT**offset * ahead, 0.0)
    targets_s[...] = target
    residual = target - value
    terms = jnp.where(residual < 0, 1.0 - EXPECTILE, EXPECTILE) * residual * residual
    loss[...] = jnp.sum(jnp.sum(terms, axis=0, keepdims=True), axis=1, keepdims=True) / (
        total_rows * LANES
    )
    own = pl.ds(rank[0] * per, per)
    values[...] = values_s[own]
    targets[...] = targets_s[own]


def per_device(
    states,
    inner_weight,
    gate_weight,
    state_weight,
    step_weight,
    step_bias,
    decay_rate,
    skip_gain,
    conv_inner,
    conv_state,
    norm_gain,
    value_weight,
    rewards,
    done_flags,
    horizon,
):
    length = states.shape[0]
    heads = step_bias.shape[0]
    inner_width = inner_weight.shape[1]
    state_width = state_weight.shape[1]
    shards = lax.axis_size("seq")
    devices = shards * lax.axis_size("head")
    depth = heads * LANES // shards
    per = length // LANES
    rank = lax.axis_index("seq").astype(jnp.int32).reshape(1)
    shape = jax.ShapeDtypeStruct
    done_row = done_flags.reshape(1, length)

    halo = lax.ppermute(
        states[length - HALO :], "seq", [(i, i + 1) for i in range(shards - 1)]
    )
    inner_pre, state_pre, rows, cols = call(
        project_body,
        [
            shape((length, inner_width), BF16),
            shape((length, state_width), BF16),
            shape((3 * heads, length), F32),
            shape((length, LANES), F32),
        ],
        [SMEM, SMEM] + [VMEM] * 5,
        [pltpu.VMEM((length, LANES), F32)],
        flops=2 * length * states.shape[1] * (inner_width + state_width),
        name="project",
    )(step_bias, decay_rate, done_row, states, inner_weight, state_weight, step_weight)
    inner, state, message = call(
        conv_body,
        [
            shape((length, inner_width), BF16),
            shape((length, state_width), BF16),
            shape((shards, depth + 2 * heads + SERIES, LANES), BF16),
        ],
        [VMEM] * 12,
        [pltpu.VMEM((2, length + HALO, LANES), F32), pltpu.VMEM((length, inner_width), BF16)],
        flops=length * inner_width * 600,
        name="conv",
    )(
        halo,
        inner_weight,
        state_weight,
        inner_pre,
        state_pre,
        conv_inner,
        conv_state,
        rows,
        cols,
        rewards.reshape(1, length),
        done_row,
        horizon.reshape(1, length),
    )
    received = lax.all_to_all(message, "seq", 0, 0, tiled=True)
    gate = call(
        gate_body,
        shape((length, inner_width), F32),
        [VMEM, VMEM, ANY],
        flops=2 * length * states.shape[1] * inner_width,
        name="gate",
    )(states, gate_weight, message)
    carried = call(
        scan_body,
        shape((shards, depth, LANES), BF16),
        [SMEM, VMEM],
        name="scan",
    )(rank, received)
    entered = lax.all_to_all(carried, "seq", 0, 0, tiled=True).reshape(heads * LANES, LANES)
    trajectory = shape((shards * per, LANES), F32)
    local, returns, code = call(
        inside_body,
        [shape((length, inner_width), F32), trajectory, trajectory],
        [SMEM] + [VMEM] * 5,
        [pltpu.VMEM((length, length), F32)] + [pltpu.VMEM((shards * per, LANES), F32)] * 3,
        flops=length * length * inner_width * 4,
        name="inside",
    )(skip_gain, inner, state, rows, cols, received)
    parts = call(
        finish_body,
        shape((devices, 2 * per, LANES), F32),
        [VMEM] * 7,
        flops=length * inner_width * 300,
        name="finish",
    )(
        state,
        entered,
        local,
        gate,
        cols,
        norm_gain.reshape(1, inner_width),
        value_weight.reshape(1, inner_width),
    )
    everything = lax.all_to_all(parts, ("seq", "head"), 0, 0, tiled=True)
    own = shape((per, LANES), F32)
    values, targets, value_loss = call(
        loss_body,
        [own, own, shape((1, 1), F32)],
        [SMEM] + [VMEM] * 3,
        [pltpu.VMEM((shards * per, LANES), F32)] * 2,
        name="loss",
    )(rank, everything, returns, code)
    return values.reshape(length), targets.reshape(length), value_loss.reshape(())


def solution(mesh):
    placed = (
        P("seq", None),
        P(None, "head"),
        P(None, "head"),
        P(),
        P(None, "head"),
        P("head"),
        P("head"),
        P("head"),
        P(None, "head"),
        P(),
        P("head"),
        P("head"),
        P("seq"),
        P("seq"),
        P("seq"),
    )
    return jax.shard_map(
        per_device, mesh=mesh, in_specs=placed, out_specs=(P("seq"), P("seq"), P()), check_vma=False
    )
```

time: 175 us -> 77.2 us (0.44)
  blocking collectives: 54 us -> 14.3 us
  Pallas kernels: 0 us -> 32.9 us
  matrix products: 26.7 us -> 0 us
  other arithmetic: 24.9 us -> 0 us
  starting transfers between devices: 29.3 us -> 13.3 us
  local copies, waits for them, and re-layouts: 17.5 us -> 4.6 us
  waiting for transfers between devices: 17.6 us -> 10.7 us
  between operations: 4.12 us -> 0.66 us
    psum x3 -> x0, blocking collectives: 35.3 us -> none  [the longest x1 23 us: per_device(): lax.psum(local_loss, 'seq') / (token_count * lax.axis_size('seq'))]
    pallas_call x0 -> x7, Pallas kernels: none -> 32.9 us  [the longest x1 7.69 us: per_device(): call(project_body, [shape((length, inner_width), BF16), shape((length, st...]
    dot_general x13 -> x0, matrix products: 26.7 us -> none  [the longest x1 5.87 us: per_device(): jnp.dot(states, inner_weight, preferred_element_type=jnp.float32)]
    ppermute x6 -> x1, starting transfers between devices: 29.3 us -> 4.86 us  [per_device(): lax.ppermute(states[length - HALO:], 'seq', [(i, i + 1) for i in range(sh...]
    all_gather x1 -> x0, blocking collectives: 18.7 us -> none  [per_device(): everyone = lax.all_gather(device_decay[None, :], 'seq', axis=0, tiled=True)]
    ppermute x6 -> x1, waiting for transfers between devices: 17.6 us -> 0.01 us  [per_device(): lax.ppermute(states[length - HALO:], 'seq', [(i, i + 1) for i in range(sh...]
    all_to_all x0 -> x1, blocking collectives: none -> 14.3 us  [per_device(): everything = lax.all_to_all(parts, ('seq', 'head'), 0, 0, tiled=True)]
    all_to_all x0 -> x2, waiting for transfers between devices: none -> 10.7 us  [the longest x1 10.7 us: per_device(): received = lax.all_to_all(message, 'seq', 0, 0, tiled=True)]
  transfers between devices with their start and end apart: 6 -> 3, of which waited for: 5 -> 1; matrix products, arithmetic and copies ran while one was open for 17% -> 2% of each run, Pallas kernels for 0% -> 25%
where the time goes in v1:
time: 77.2 us; the launch traced here: 76.6 us
  Pallas kernels  32.9 us (43%)
  blocking collectives  14.3 us (19%)
  starting transfers between devices  13.3 us (17%)
  waiting for transfers between devices  10.7 us (14%)
  local copies, waits for them, and re-layouts  4.6 us (6%)
    all_to_all x1, blocking collectives, per_device(): everything = lax.all_to_all(parts, ('seq', 'head'), 0, 0, tiled=True)  14.3 us
    all_to_all x1, waiting for transfers between devices, per_device(): received = lax.all_to_all(message, 'seq', 0, 0, tiled=True)  10.7 us
    pallas_call x1, Pallas kernels, per_device(): call(project_body, [shape((length, inner_width), BF16), shape((length, st...  7.69 us
    pallas_call x1, Pallas kernels, per_device(): call(gate_body, shape((length, inner_width), F32), [VMEM, VMEM, ANY], flo...  6.59 us
    pallas_call x1, Pallas kernels, per_device(): call(conv_body, [shape((length, inner_width), BF16), shape((length, state...  6.45 us
    all_to_all x1, starting transfers between devices, per_device(): received = lax.all_to_all(message, 'seq', 0, 0, tiled=True)  4.88 us
    ppermute x1, starting transfers between devices, per_device(): lax.ppermute(states[length - HALO:], 'seq', [(i, i + 1) for i in range(sh...  4.86 us
    pallas_call x1, Pallas kernels, per_device(): call(inside_body, [shape((length, inner_width), F32), trajectory, traject...  4.7 us
  transfers between devices with their start and end apart: 3, of which 1 were waited for; matrix products, arithmetic and copies ran while one was open for 2% of the time, Pallas kernels for 25%

profile of v1, /device:TPU:0, one launch (start us, length us, event | category | flops | bytes accessed | tf_op | source)
XLA Modules:
  0.0 76.6 jit_solution(14971951643205053559)
XLA Ops:
  0.6 0.8 slice.3
  1.4 4.9 %collective-permute-start = (bf16[8,2048]{1,0:T(8,128)(2,1)S(1)}, bf16[8,2048]{1,0:T(8,128)(2,1)S(1)}, u32[]{:S(2)}, u32[]{:S(2)}) collective-permute-start(bf16[8,2048]{1,0:T(8,128)(2,1)S(1)} %slice.3), channel_id=1, source_target_pairs={{0,4},{4,8},{8,12},{12,16},{16,20},{20,24},{24,28},{1,5},{5,9},{9,... | collective-permute-start | bytes 98312 | tf_op jit(solution)/shard_map/ppermute | solution.py:327
  6.3 1.8 %copy.18.step_w = bf16[2048,8]{1,0:T(8,128)(2,1)} copy(bf16[2048,8]{0,1:T(8,128)(2,1)} %param.19) | data formatting | bytes 65536 | tf_op args[4]
  8.0 7.7 %project.1 = (bf16[512,1024]{1,0:T(8,128)(2,1)}, bf16[512,256]{1,0:T(8,128)(2,1)}, f32[24,512]{1,0:T(8,128)}, f32[512,128]{1,0:T(8,128)}) custom-call(f32[8]{0:T(128)} %bias.1, f32[8]{0:T(128)} %decay.1, s32[1,512]{1,0:T(1,128)} %bitcast.13, bf16[512,2048]{1,0:T(8,128)(2,1)} %states.3, bf16[2048,1024]{1,0:T(8,128)(2,1)} %inner_w.3, ...), custom_call_target="tpu_custom_call" | custom-call | flops 2684354560 | tf_op jit(solution)/shard_map/project/pallas_call | solution.py:330
  15.7 0.0 collective-permute-done.halo
  15.7 0.0 copy-start.2
  15.8 0.6 copy-done.2
  16.3 6.5 %conv.1 = (bf16[512,1024]{1,0:T(8,128)(2,1)}, bf16[512,256]{1,0:T(8,128)(2,1)}, bf16[8,176,128]{2,1,0:T(8,128)(2,1)}) custom-call(bf16[8,2048]{1,0:T(8,128)(2,1)} %copy-done.2, bf16[2048,1024]{1,0:T(8,128)(2,1)} %inner_w.3, bf16[2048,256]{1,0:T(8,128)(2,1)} %state_w.3, bf16[512,1024]{1,0:T(8,128)(2,1)} %get-tuple-element.16.inner_pre, ...), custom_call_target="tpu_custom_call" | custom-call | flops 314572800 | tf_op jit(solution)/shard_map/conv/pallas_call | solution.py:343
  22.8 4.9 %all-to-all-start = ((bf16[8,176,128]{2,1,0:T(8,128)(2,1)}), bf16[8,176,128]{2,1,0:T(8,128)(2,1)S(1)}, u32[]{:S(2)}, u32[]{:S(2)}) async-start(bf16[8,176,128]{2,1,0:T(8,128)(2,1)} %get-tuple-element.21.after), calls=%async_computation | async-start | bytes 720896 | tf_op jit(solution)/shard_map/all_to_all | solution.py:368
  27.7 10.7 %all-to-all-done.received = bf16[8,176,128]{2,1,0:T(8,128)(2,1)S(1)} async-done(((bf16[8,176,128]{2,1,0:T(8,128)(2,1)}), bf16[8,176,128]{2,1,0:T(8,128)(2,1)S(1)}, u32[]{:S(2)}, u32[]{:S(2)}) %all-to-all-start) | async-done | bytes 360480 | tf_op jit(solution)/shard_map/all_to_all | solution.py:368
  38.4 0.0 copy-start
  38.4 0.8 copy-done
  39.2 1.8 %scan.1 = bf16[8,128,128]{2,1,0:T(8,128)(2,1)} custom-call(s32[1]{0:T(128)} %bitcast.rank, bf16[8,176,128]{2,1,0:T(8,128)(2,1)} %copy-done), custom_call_target="tpu_custom_call" | custom-call | tf_op jit(solution)/shard_map/scan/pallas_call | solution.py:376
  40.9 3.6 %all-to-all-start.1 = ((bf16[8,128,128]{2,1,0:T(8,128)(2,1)}), bf16[8,128,128]{2,1,0:T(8,128)(2,1)S(1)}, u32[]{:S(2)}, u32[]{:S(2)}) async-start(bf16[8,128,128]{2,1,0:T(8,128)(2,1)} %scan.1), calls=%async_computation.1 | async-start | bytes 524288 | tf_op jit(solution)/shard_map/all_to_all | solution.py:382
  44.5 6.6 %gate.1 = f32[512,1024]{1,0:T(8,128)} custom-call(bf16[512,2048]{1,0:T(8,128)(2,1)} %states.3, bf16[2048,1024]{1,0:T(8,128)(2,1)} %gate_w.1, bf16[8,176,128]{2,1,0:T(8,128)(2,1)} %get-tuple-element.21.after), custom_call_target="tpu_custom_call" | custom-call | flops 2147483648 | tf_op jit(solution)/shard_map/gate/pallas_call | solution.py:369
  51.1 4.7 %inside.1 = (f32[512,1024]{1,0:T(8,128)}, f32[32,128]{1,0:T(8,128)}, f32[32,128]{1,0:T(8,128)}) custom-call(f32[8]{0:T(128)} %skip.1, bf16[512,1024]{1,0:T(8,128)(2,1)} %get-tuple-element.22.inner, bf16[512,256]{1,0:T(8,128)(2,1)} %get-tuple-element.20.state, f32[24,512]{1,0:T(8,128)} %get-tuple-element.18.rows, f32[512,128]{1,0:T(8,128)} %get-tuple-element.19.cols, ...), custom_call_target="tpu_custom_call" | custom-call | flops 1073741824 | tf_op jit(solution)/shard_map/inside/pallas_call | solution.py:384
  55.8 0.0 all-to-all-done.1
  55.8 0.0 copy-start.1
  55.8 0.7 copy-done.1
  56.5 4.1 %finish.1 = f32[32,8,128]{2,1,0:T(8,128)} custom-call(bf16[512,256]{1,0:T(8,128)(2,1)} %get-tuple-element.20.state, bf16[1024,128]{1,0:T(8,128)(2,1)} %bitcast.10, f32[512,1024]{1,0:T(8,128)} %get-tuple-element.23.local, f32[512,1024]{1,0:T(8,128)} %gate.1, f32[512,128]{1,0:T(8,128)} %get-tuple-element.19.cols, f32[1,1024]{1,0:T(1,128)} %bitcast.11, ...), custom_call_target="tpu_custom_call" | custom-call | flops 157286400 | tf_op jit(solution)/shard_map/finish/pallas_call | solution.py:392
  60.6 14.3 %all_to_all.15.received = f32[32,8,128]{2,1,0:T(8,128)} all-to-all(f32[32,8,128]{2,1,0:T(8,128)} %finish.1), channel_id=1, replica_groups=mesh['seq'=8,'head'=4] {'seq','head'}, dimensions={0} | all-to-all | bytes 262144 | tf_op jit(solution)/shard_map/all_to_all | solution.py:407
  74.9 1.7 %loss.1 = (f32[4,128]{1,0:T(4,128)}, f32[4,128]{1,0:T(4,128)}, f32[1,1]{1,0:T(1,128)}) custom-call(s32[1]{0:T(128)} %bitcast.rank, f32[32,8,128]{2,1,0:T(8,128)} %all_to_all.15.received, f32[32,128]{1,0:T(8,128)} %get-tuple-element.24.returns, f32[32,128]{1,0:T(8,128)} %get-tuple-element.25.code), custom_call_target="tpu_custom_call" | custom-call | tf_op jit(solution)/shard_map/loss/pallas_call | solution.py:409
Async XLA Ops:
  1.4 14.3 %collective-permute-start = (bf16[8,2048]{1,0:T(8,128)(2,1)S(1)}, bf16[8,2048]{1,0:T(8,128)(2,1)S(1)}, u32[]{:S(2)}, u32[]{:S(2)}) collective-permute-start(bf16[8,2048]{1,0:T(8,128)(2,1)S(1)} %slice.3), channel_id=1, source_target_pairs={{0,4},{4,8},{8,12},{12,16},{16,20},{20,24},{24,28},{1,5},{5,9},{9,... | collective-permute-start | bytes 98312 | tf_op jit(solution)/shard_map/ppermute | solution.py:327
  15.7 0.6 copy-start.2
  22.8 15.6 %all-to-all-start = ((bf16[8,176,128]{2,1,0:T(8,128)(2,1)}), bf16[8,176,128]{2,1,0:T(8,128)(2,1)S(1)}, u32[]{:S(2)}, u32[]{:S(2)}) async-start(bf16[8,176,128]{2,1,0:T(8,128)(2,1)} %get-tuple-element.21.after), calls=%async_computation | async-start | bytes 720896 | tf_op jit(solution)/shard_map/all_to_all | solution.py:368
  38.4 0.8 copy-start
  40.9 14.9 %all-to-all-start.1 = ((bf16[8,128,128]{2,1,0:T(8,128)(2,1)}), bf16[8,128,128]{2,1,0:T(8,128)(2,1)S(1)}, u32[]{:S(2)}, u32[]{:S(2)}) async-start(bf16[8,128,128]{2,1,0:T(8,128)(2,1)} %scan.1), calls=%async_computation.1 | async-start | bytes 524288 | tf_op jit(solution)/shard_map/all_to_all | solution.py:382
  55.8 0.7 copy-start.1

commit v2 on v1

--- a/solution.py
+++ b/solution.py
@@ -14,26 +14,30 @@
 EPSILON = 1e-05
 LANES = 128
 HALO = 8
-SERIES = 32
 RESET = 300.0
 VMEM = pl.BlockSpec(memory_space=pltpu.VMEM)
 SMEM = pl.BlockSpec(memory_space=pltpu.SMEM)
 ANY = pl.BlockSpec(memory_space=pl.ANY)
+HBM = pl.BlockSpec(memory_space=pltpu.HBM)
 F32 = jnp.float32
 BF16 = jnp.bfloat16
 
 
-def call(body, outs, ins, scratch=(), flops=0, name=None):
+def call(body, outs, ins, scratch=(), flops=0, moved=0, name=None, limit=10):
     return pl.pallas_call(
         body,
         out_shape=outs,
         in_specs=ins,
         out_specs=jax.tree.map(lambda _: VMEM, outs),
         scratch_shapes=list(scratch),
-        cost_estimate=pl.CostEstimate(flops=flops, transcendentals=0, bytes_accessed=0),
-        compiler_params=pltpu.CompilerParams(vmem_limit_bytes=60 * 2**20),
+        cost_estimate=pl.CostEstimate(flops=flops, transcendentals=0, bytes_accessed=moved),
+        compiler_params=pltpu.CompilerParams(vmem_limit_bytes=limit * 2**20),
         name=name,
     )
+
+
+def in_hbm(x):
+    return pltpu.with_memory_space_constraint(x, pltpu.HBM)
 
 
 def dot(a, b, dims=((1,), (0,))):
@@ -52,14 +56,50 @@
     return out
 
 
-def project_body(
-    bias, decay, done, states, inner_w, state_w, step_w, inner_pre, state_pre, rows, cols, raw
+def entry_body(
+    bias_hbm,
+    decay_hbm,
+    done_hbm,
+    states_hbm,
+    state_hbm,
+    step_hbm,
+    states,
+    state_w,
+    state_pre,
+    rows,
+    cols,
+    edge,
+    step_w,
+    done,
+    bias,
+    decay,
+    arrived,
 ):
     length = states.shape[0]
     heads = bias.shape[0]
-    raw[:, :heads] = dot(states[...], step_w[...])
+    pairs = [(states_hbm, states), (step_hbm, step_w), (done_hbm, done)]
+    pairs += [(bias_hbm, bias), (decay_hbm, decay), (state_hbm, state_w)]
+    copies = [pltpu.make_async_copy(*pair, arrived.at[i]) for i, pair in enumerate(pairs)]
+    for copy in copies:
+        copy.start()
+    for copy in copies:
+        copy.wait()
+    edge[...] = states[length - HALO :]
+    step_rows(bias, decay, done, states, step_w, rows, cols, heads, length)
+    width = 2 * LANES
+    for c in range(0, state_w.shape[1], width):
+        state_pre[:, c : c + width] = dot(states[...], state_w[:, c : c + width]).astype(BF16)
+
+
+def project_body(states, inner_w, inner_pre):
+    width = 2 * LANES
+    for c in range(0, inner_w.shape[1], width):
+        inner_pre[:, c : c + width] = dot(states[...], inner_w[:, c : c + width]).astype(BF16)
+
+
+def step_rows(bias, decay, done, states, step_w, rows, cols, heads, length):
     shape = (heads, length)
-    step = raw[...].T[:heads] + column(bias, heads, shape)
+    step = dot(step_w[...], states[...], ((1,), (1,))) + column(bias, heads, shape)
     step = jnp.maximum(step, 0.0) + jnp.log1p(jnp.exp(-jnp.abs(step)))
     ended = jnp.broadcast_to(done[...].astype(F32) * RESET, shape)
     total = -column(decay, heads, shape) * step - ended
@@ -76,11 +116,6 @@
     tail = jnp.exp(last - reach) * step
     fill = jnp.zeros((LANES - 3 * heads, length), F32)
     cols[...] = jnp.concatenate([tail, reach, jnp.exp(reach), fill], axis=0).T
-    width = 256
-    for c in range(0, state_w.shape[1], width):
-        state_pre[:, c : c + width] = dot(states[...], state_w[:, c : c + width]).astype(BF16)
-    for c in range(0, inner_w.shape[1], width):
-        inner_pre[:, c : c + width] = dot(states[...], inner_w[:, c : c + width]).astype(BF16)
 
 
 def conv_body(
@@ -104,7 +139,8 @@
 ):
     length = inner_pre.shape[0]
     heads = rows.shape[0] // 3
-    shards, depth = message.shape[0], message.shape[1] - 2 * heads - SERIES
+    shards = message.shape[0]
+    depth = heads * LANES // shards
     block = LANES
 
     def convolve(rim, source, taps, target, c, scaled):
@@ -142,83 +178,62 @@
                 message[dest, at_row : at_row + step] = own[q : q + step]
     total = rows[2 * heads :, 0:LANES]
     high = total.astype(BF16).astype(F32)
-    per_row = length // LANES
-    split = lambda ref: [ref[:, q * LANES : (q + 1) * LANES].astype(F32) for q in range(per_row)]
-    reward = split(rewards)
-    first = [r.astype(BF16).astype(F32) for r in reward]
-    second = [(r - a).astype(BF16).astype(F32) for r, a in zip(reward, first)]
-    third = [r - a - b for r, a, b in zip(reward, first, second)]
-    stack = first + second + third + split(done) + split(horizon)
-    stack.append(jnp.zeros((SERIES - len(stack), LANES), F32))
-    extra = jnp.concatenate([high, total - high] + stack, axis=0).astype(BF16)
+    low = total - high
+    per = length // LANES
+    reward = lane_rows(rewards, per)
+    first = reward.astype(BF16).astype(F32)
+    second = (reward - first).astype(BF16).astype(F32)
+    series = [first, second, reward - first - second, lane_rows(done, per), lane_rows(horizon, per)]
+    held = max(1, depth // LANES)
+    spare = message.shape[1] - depth - 5 * per - 2 * held
+    if spare:
+        series.append(jnp.zeros((spare, LANES), F32))
     for dest in range(shards):
-        message[dest, depth:] = extra
-
-
-def gate_body(states, gate_w, after, gate):
-    del after
-    width = 256
+        head = dest * depth // LANES
+        decays = [high[head : head + held], low[head : head + held]]
+        message[dest, depth:] = jnp.concatenate(series + decays, axis=0).astype(BF16)
+
+
+def lane_rows(ref, count):
+    pieces = [ref[:, q * LANES : (q + 1) * LANES].astype(F32) for q in range(count)]
+    return jnp.concatenate(pieces, axis=0)
+
+
+def gate_body(
+    rank,
+    states_hbm,
+    gate_hbm,
+    received,
+    after,
+    gate,
+    returns,
+    code,
+    states,
+    gate_w,
+    reward_s,
+    alive_s,
+    steps_s,
+    arrived,
+):
+    del rank
+    pairs = [(gate_hbm, gate_w), (states_hbm, states)]
+    copies = [pltpu.make_async_copy(*pair, arrived.at[i]) for i, pair in enumerate(pairs)]
+    for copy in copies:
+        copy.start()
+    depth = after.shape[1]
+    series(received, depth, states.shape[0] // LANES, returns, code, reward_s, alive_s, steps_s)
+    for copy in copies:
+        copy.wait()
+    width = 2 * LANES
     for c in range(0, gate_w.shape[1], width):
         pre = dot(states[...], gate_w[:, c : c + width]).astype(BF16).astype(F32)
-        gate[:, c : c + width] = silu(pre)
-
-
-def scan_body(rank, received, carried):
-    shards, depth = carried.shape[0], carried.shape[1]
-    heads = shards * depth // LANES
-    part = min(depth, LANES)
-    row = lax.broadcasted_iota(jnp.int32, (2 * heads, LANES), 0)
-    for q in range(0, depth, part):
-        head = lax.div(rank[0] * depth + q, LANES)
-        state = jnp.zeros((part, LANES), F32)
-        for j in range(shards):
-            carried[j, q : q + part] = state.astype(BF16)
-            both = received[j, depth : depth + 2 * heads].astype(F32)
-            keep = (row == head) | (row == head + heads)
-            decay = jnp.sum(jnp.where(keep, both, 0.0), axis=0, keepdims=True)
-            state = decay * state + received[j, q : q + part].astype(F32)
-
-
-def shift_time(x, distance):
-    lane = lax.broadcasted_iota(jnp.int32, x.shape, 1)
-    row = lax.broadcasted_iota(jnp.int32, x.shape, 0)
-    count = x.shape[0]
-    below = jnp.where(row < count - 1, pltpu.roll(x, count - 1, 0), 0.0)
-    moved = jnp.where(lane < distance, below, x)
-    return pltpu.roll(moved, LANES - distance, 1)
-
-
-def inside_body(
-    skip, inner, state, rows, cols, received, local, returns, code, scores, reward_s, alive_s, steps_s
-):
-    length = inner.shape[0]
-    heads = rows.shape[0] // 3
-    block = LANES
-    readout = state[:, LANES:]
-    writes = state[:, :LANES]
-    scores[...] = dot(readout, writes, ((1,), (1,)))
-    below = lax.broadcasted_iota(jnp.int32, (block, block), 0) >= lax.broadcasted_iota(
-        jnp.int32, (block, block), 1
-    )
-    for h in range(heads):
-        at = slice(h * LANES, (h + 1) * LANES)
-        for r in range(0, length, block):
-            here = jnp.broadcast_to(cols[r : r + block, heads + h : heads + h + 1], (block, LANES))
-            pieces = []
-            for s in range(0, r + block, block):
-                gap = here - rows[h : h + 1, s : s + block]
-                if s == r:
-                    gap = jnp.where(below, gap, -jnp.inf)
-                weight = scores[r : r + block, s : s + block] * rows[heads + h : heads + h + 1, s : s + block]
-                pieces.append((jnp.exp(gap) * weight).astype(BF16))
-            weights = jnp.concatenate(pieces, axis=1)
-            out = dot(weights, inner[0 : r + block, at])
-            local[r : r + block, at] = out + skip[h] * inner[r : r + block, at].astype(F32)
+        gate[:, c : c + width] = silu(pre).astype(gate.dtype)
+
+
+def series(received, depth, per, returns, code, reward_s, alive_s, steps_s):
     shards = received.shape[0]
-    series = received.shape[1] - SERIES
-    per = length // LANES
     for j in range(shards):
-        extra = received[j, series:].astype(F32)
+        extra = received[j, depth:].astype(F32)
         to = slice(j * per, (j + 1) * per)
         reward_s[to] = extra[0:per] + extra[per : 2 * per] + extra[2 * per : 3 * per]
         alive_s[to] = 1.0 - extra[3 * per : 4 * per]
@@ -235,6 +250,60 @@
             survive = survive * (shift_time(alive, offset) if offset else alive)
     returns[...] = gained
     code[...] = reached
+
+
+def scan_body(received, after, carried):
+    del after
+    shards, depth = carried.shape[0], carried.shape[1]
+    held = max(1, depth // LANES)
+    part = min(depth, LANES)
+    end = received.shape[1]
+    for q in range(held):
+        state = jnp.zeros((part, LANES), F32)
+        for j in range(shards):
+            carried[j, q * part : (q + 1) * part] = state.astype(BF16)
+            both = received[j, depth:end].astype(F32)
+            high = both[end - depth - 2 * held + q : end - depth - 2 * held + q + 1]
+            low = both[end - depth - held + q : end - depth - held + q + 1]
+            state = (high + low) * state + received[j, q * part : (q + 1) * part].astype(F32)
+
+
+def shift_time(x, distance):
+    lane = lax.broadcasted_iota(jnp.int32, x.shape, 1)
+    row = lax.broadcasted_iota(jnp.int32, x.shape, 0)
+    count = x.shape[0]
+    below = jnp.where(row < count - 1, pltpu.roll(x, count - 1, 0), 0.0)
+    moved = jnp.where(lane < distance, below, x)
+    return pltpu.roll(moved, LANES - distance, 1)
+
+
+def inside_body(
+    skip, inner, state, rows, cols, local, scores
+):
+    length = inner.shape[0]
+    heads = rows.shape[0] // 3
+    block = LANES
+    readout = state[:, LANES:]
+    writes = state[:, :LANES]
+    scores[...] = dot(readout, writes, ((1,), (1,)))
+    below = lax.broadcasted_iota(jnp.int32, (block, block), 0) >= lax.broadcasted_iota(
+        jnp.int32, (block, block), 1
+    )
+    for h in range(heads):
+        at = slice(h * LANES, (h + 1) * LANES)
+        for r in range(0, length, block):
+            here = jnp.broadcast_to(cols[r : r + block, heads + h : heads + h + 1], (block, LANES))
+            pieces = []
+            for s in range(0, r + block, block):
+                gap = here - rows[h : h + 1, s : s + block]
+                if s == r:
+                    gap = jnp.where(below, gap, -jnp.inf)
+                weight = scores[r : r + block, s : s + block] * rows[heads + h : heads + h + 1, s : s + block]
+                pieces.append((jnp.exp(gap) * weight).astype(BF16))
+            weights = jnp.concatenate(pieces, axis=1)
+            out = dot(weights, inner[0 : r + block, at])
+            out = out + skip[h] * inner[r : r + block, at].astype(F32)
+            local[r : r + block, at] = out.astype(local.dtype)
 
 
 def finish_body(state, carried, local, gate, cols, norm_gain, value_weight, message):
@@ -256,8 +325,8 @@
                 h = c + i
                 at = slice(h * LANES, (h + 1) * LANES)
                 reach = cols[r : r + block, 2 * heads + h : 2 * heads + h + 1]
-                mixed = local[r : r + block, at] + reach * fix[:, i * LANES : (i + 1) * LANES]
-                gated = mixed * gate[r : r + block, at]
+                mixed = local[r : r + block, at].astype(F32) + reach * fix[:, i * LANES : (i + 1) * LANES]
+                gated = mixed * gate[r : r + block, at].astype(F32)
                 square = square + gated * gated
                 total = total + gated * weight[:, at]
         squares.append(jnp.sum(square.T, axis=0, keepdims=True))
@@ -320,32 +389,54 @@
     devices = shards * lax.axis_size("head")
     depth = heads * LANES // shards
     per = length // LANES
+    packed = -(-(5 * per + 2 * max(1, depth // LANES)) // 8) * 8
     rank = lax.axis_index("seq").astype(jnp.int32).reshape(1)
     shape = jax.ShapeDtypeStruct
     done_row = done_flags.reshape(1, length)
 
-    halo = lax.ppermute(
-        states[length - HALO :], "seq", [(i, i + 1) for i in range(shards - 1)]
-    )
-    inner_pre, state_pre, rows, cols = call(
-        project_body,
+    states_near, state_weight, state_pre, rows, cols, edge = call(
+        entry_body,
         [
-            shape((length, inner_width), BF16),
+            shape(states.shape, BF16),
+            shape(state_weight.shape, BF16),
             shape((length, state_width), BF16),
             shape((3 * heads, length), F32),
             shape((length, LANES), F32),
+            shape((HALO, states.shape[1]), BF16),
         ],
-        [SMEM, SMEM] + [VMEM] * 5,
-        [pltpu.VMEM((length, LANES), F32)],
-        flops=2 * length * states.shape[1] * (inner_width + state_width),
+        [HBM] * 6,
+        [
+            pltpu.VMEM(step_weight.shape[::-1], BF16),
+            pltpu.VMEM((1, length), jnp.int32),
+            pltpu.SMEM((heads,), F32),
+            pltpu.SMEM((heads,), F32),
+            pltpu.SemaphoreType.DMA((6,)),
+        ],
+        flops=2 * length * states.shape[1] * inner_width,
+        moved=4 * states.size,
+        name="entry",
+    )(
+        in_hbm(step_bias),
+        in_hbm(decay_rate),
+        in_hbm(done_row),
+        in_hbm(states),
+        in_hbm(state_weight),
+        in_hbm(step_weight.T),
+    )
+    halo = lax.ppermute(edge, "seq", [(i, i + 1) for i in range(shards - 1)])
+    inner_pre = call(
+        project_body,
+        shape((length, inner_width), BF16),
+        [VMEM, VMEM],
+        flops=2 * length * states.shape[1] * inner_width,
         name="project",
-    )(step_bias, decay_rate, done_row, states, inner_weight, state_weight, step_weight)
+    )(states_near, inner_weight)
     inner, state, message = call(
         conv_body,
         [
             shape((length, inner_width), BF16),
             shape((length, state_width), BF16),
-            shape((shards, depth + 2 * heads + SERIES, LANES), BF16),
+            shape((shards, depth + packed, LANES), BF16),
         ],
         [VMEM] * 12,
         [pltpu.VMEM((2, length + HALO, LANES), F32), pltpu.VMEM((length, inner_width), BF16)],
@@ -366,29 +457,32 @@
         horizon.reshape(1, length),
     )
     received = lax.all_to_all(message, "seq", 0, 0, tiled=True)
-    gate = call(
-        gate_body,
-        shape((length, inner_width), F32),
-        [VMEM, VMEM, ANY],
-        flops=2 * length * states.shape[1] * inner_width,
-        name="gate",
-    )(states, gate_weight, message)
+    local = call(
+        inside_body,
+        shape((length, inner_width), BF16),
+        [SMEM] + [VMEM] * 4,
+        [pltpu.VMEM((length, length), F32)],
+        flops=length * length * inner_width * 4,
+        name="inside",
+    )(skip_gain, inner, state, rows, cols)
     carried = call(
         scan_body,
         shape((shards, depth, LANES), BF16),
-        [SMEM, VMEM],
+        [VMEM, ANY],
         name="scan",
-    )(rank, received)
+    )(received, local)
     entered = lax.all_to_all(carried, "seq", 0, 0, tiled=True).reshape(heads * LANES, LANES)
     trajectory = shape((shards * per, LANES), F32)
-    local, returns, code = call(
-        inside_body,
-        [shape((length, inner_width), F32), trajectory, trajectory],
-        [SMEM] + [VMEM] * 5,
-        [pltpu.VMEM((length, length), F32)] + [pltpu.VMEM((shards * per, LANES), F32)] * 3,
-        flops=length * length * inner_width * 4,
-        name="inside",
-    )(skip_gain, inner, state, rows, cols, received)
+    gate, returns, code = call(
+        gate_body,
+        [shape((length, inner_width), BF16), trajectory, trajectory],
+        [SMEM, HBM, HBM, VMEM, ANY],
+        [pltpu.VMEM(states.shape, BF16), pltpu.VMEM(gate_weight.shape, BF16)]
+        + [pltpu.VMEM((shards * per, LANES), F32)] * 3
+        + [pltpu.SemaphoreType.DMA((2,))],
+        flops=2 * length * states.shape[1] * inner_width,
+        name="gate",
+    )(rank, in_hbm(states), in_hbm(gate_weight), received, carried)
     parts = call(
         finish_body,
         shape((devices, 2 * per, LANES), F32),

time: 77.2 us -> 56.2 us (0.73)
  Pallas kernels: 32.9 us -> 19.4 us
  local copies, waits for them, and re-layouts: 4.6 us -> 0.05 us
  blocking collectives: 14.3 us -> 11.5 us
  starting transfers between devices: 13.3 us -> 14.5 us
  waiting for transfers between devices: 10.7 us -> 9.52 us
    pallas_call x4 -> x5, Pallas kernels: 20.7 us -> 14.3 us  [the longest x1 5.35 us: per_device(): call(gate_body, [shape((length, inner_width), BF16), trajectory, trajecto...]
    all_to_all x1, waiting for transfers between devices: 10.7 us -> 6.43 us  [per_device(): received = lax.all_to_all(message, 'seq', 0, 0, tiled=True)]
    unnamed x7 -> x18, local copies, waits for them, and re-layouts: 3.84 us -> 0.05 us
    pallas_call x1, Pallas kernels: 6.45 us -> 3.31 us  [per_device(): call(conv_body, [shape((length, inner_width), BF16), shape((length, state...]
    all_to_all x1, waiting for transfers between devices: 0.01 us -> 3.09 us  [per_device(): lax.all_to_all(carried, 'seq', 0, 0, tiled=True)]
    pallas_call x1, Pallas kernels: 4.06 us -> 1.02 us  [per_device(): call(finish_body, shape((devices, 2 * per, LANES), F32), [VMEM] * 7, flop...]
    all_to_all x1, blocking collectives: 14.3 us -> 11.5 us  [per_device(): everything = lax.all_to_all(parts, ('seq', 'head'), 0, 0, tiled=True)]
    all_to_all x1, starting transfers between devices: 4.88 us -> 5.82 us  [per_device(): received = lax.all_to_all(message, 'seq', 0, 0, tiled=True)]
  transfers between devices with their start and end apart: 3 -> 3, of which waited for: 1 -> 2; matrix products, arithmetic and copies ran while one was open for 2% -> 0% of each run, Pallas kernels for 25% -> 18%
where the time goes in v2:
time: 56.2 us; the launch traced here: 55.8 us
  Pallas kernels  19.4 us (35%)
  starting transfers between devices  14.5 us (26%)
  blocking collectives  11.5 us (20%)
  waiting for transfers between devices  9.52 us (17%)
  between operations  0.8 us (1%)
    all_to_all x1, blocking collectives, per_device(): everything = lax.all_to_all(parts, ('seq', 'head'), 0, 0, tiled=True)  11.5 us
    all_to_all x1, waiting for transfers between devices, per_device(): received = lax.all_to_all(message, 'seq', 0, 0, tiled=True)  6.43 us
    all_to_all x1, starting transfers between devices, per_device(): received = lax.all_to_all(message, 'seq', 0, 0, tiled=True)  5.82 us
    pallas_call x1, Pallas kernels, per_device(): call(gate_body, [shape((length, inner_width), BF16), trajectory, trajecto...  5.35 us
    ppermute x1, starting transfers between devices, per_device(): halo = lax.ppermute(edge, 'seq', [(i, i + 1) for i in range(shards - 1)])  5 us
    all_to_all x1, starting transfers between devices, per_device(): lax.all_to_all(carried, 'seq', 0, 0, tiled=True)  3.7 us
    pallas_call x1, Pallas kernels, per_device(): call(entry_body, [shape(states.shape, BF16), shape(state_weight.shape, BF...  3.5 us
    pallas_call x1, Pallas kernels, per_device(): call(conv_body, [shape((length, inner_width), BF16), shape((length, state...  3.31 us
  transfers between devices with their start and end apart: 3, of which 2 were waited for; matrix products, arithmetic and copies ran while one was open for 0% of the time, Pallas kernels for 18%

profile of v2, /device:TPU:0, one launch (start us, length us, event | category | flops | bytes accessed | tf_op | source)
XLA Modules:
  0.0 55.8 jit_solution(7898370028170344553)
XLA Ops:
  0.6 0.0 copy-start
  0.6 3.5 %entry.1 = (bf16[512,2048]{1,0:T(8,128)(2,1)S(1)}, bf16[2048,256]{1,0:T(8,128)(2,1)S(1)}, bf16[512,256]{1,0:T(8,128)(2,1)S(1)}, f32[24,512]{1,0:T(8,128)S(1)}, f...) custom-call(f32[8]{0:T(128)} %bias_hbm.1, f32[8]{0:T(128)} %decay_hbm.1, s32[1,512]{1,0:T(1,128)} %bitcast.14, ...), custom_call_target="tpu_custom_call" | custom-call | flops 2147483648 | bytes 4194304 | tf_op jit(solution)/shard_map/entry/pallas_call | solution.py:397
  4.2 0.0 copy-start.1
  4.2 0.0 copy-start.2
  4.2 0.0 copy-start.5
  4.2 0.0 copy-start.6
  4.2 0.0 copy-start.7
  4.2 5.0 %collective-permute-start = (bf16[8,2048]{1,0:T(8,128)(2,1)S(1)}, bf16[8,2048]{1,0:T(8,128)(2,1)S(1)}, u32[]{:S(2)}, u32[]{:S(2)}) collective-permute-start(bf16[8,2048]{1,0:T(8,128)(2,1)S(1)} %get-tuple-element.18), channel_id=1, source_target_pairs={{0,4},{4,8},{8,12},{12,16},{16,20},{20,24},{24,28},{1,5},{5,9},{9,... | collective-permute-start | bytes 98312 | tf_op jit(solution)/shard_map/ppermute | solution.py:426
  9.2 0.0 copy-done
  9.2 2.3 %project.1.inner_pre = bf16[512,1024]{1,0:T(8,128)(2,1)S(1)} custom-call(bf16[512,2048]{1,0:T(8,128)(2,1)S(1)} %get-tuple-element.20.states, bf16[2048,1024]{1,0:T(8,128)(2,1)S(1)} %copy-done), custom_call_target="tpu_custom_call" | custom-call | flops 2147483648 | tf_op jit(solution)/shard_map/project/pallas_call | solution.py:427
  11.6 0.0 copy-start.8
  11.6 0.0 collective-permute-done.halo
  11.6 0.0 copy-done.1
  11.6 0.0 copy-done.2
  11.6 0.0 copy-done.5
  11.6 0.0 copy-done.6
  11.6 0.0 copy-done.7
  11.6 3.3 %conv.1 = (bf16[512,1024]{1,0:T(8,128)(2,1)S(1)}, bf16[512,256]{1,0:T(8,128)(2,1)S(1)}, bf16[8,152,128]{2,1,0:T(8,128)(2,1)}) custom-call(bf16[8,2048]{1,0:T(8,128)(2,1)S(1)} %collective-permute-done.halo, bf16[2048,1024]{1,0:T(8,128)(2,1)S(1)} %copy-done, bf16[2048,256]{1,0:T(8,128)(2,1)S(1)} %get-tuple-element.19.state_w, ...), custom_call_target="tpu_custom_call" | custom-call | flops 314572800 | tf_op jit(solution)/shard_map/conv/pallas_call | solution.py:434
  15.0 5.8 %all-to-all-start = ((bf16[8,152,128]{2,1,0:T(8,128)(2,1)}), bf16[8,152,128]{2,1,0:T(8,128)(2,1)S(1)}, u32[]{:S(2)}, u32[]{:S(2)}) async-start(bf16[8,152,128]{2,1,0:T(8,128)(2,1)} %get-tuple-element.25), calls=%async_computation | async-start | bytes 622592 | tf_op jit(solution)/shard_map/all_to_all | solution.py:459
  20.8 0.0 copy-done.8
  20.8 2.4 %inside.1.after.local = bf16[512,1024]{1,0:T(8,128)(2,1)S(1)} custom-call(f32[8]{0:T(128)S(1)} %copy-done.8, bf16[512,1024]{1,0:T(8,128)(2,1)S(1)} %get-tuple-element.26.inner, bf16[512,256]{1,0:T(8,128)(2,1)S(1)} %get-tuple-element.24.state, f32[24,512]{1,0:T(8,128)S(1)} %get-tuple-element.22.rows, f32[512,128]{1,0:T(8,128)S(1)} %get-tuple-element.23.cols), custom_call_target="tpu_custom_call" | custom-call | flops 1073741824 | tf_op jit(solution)/shard_map/inside/pallas_call | solution.py:460
  23.2 6.4 %all-to-all-done.received = bf16[8,152,128]{2,1,0:T(8,128)(2,1)S(1)} async-done(((bf16[8,152,128]{2,1,0:T(8,128)(2,1)}), bf16[8,152,128]{2,1,0:T(8,128)(2,1)S(1)}, u32[]{:S(2)}, u32[]{:S(2)}) %all-to-all-start) | async-done | bytes 311328 | tf_op jit(solution)/shard_map/all_to_all | solution.py:459
  29.6 0.7 %scan.1.after = bf16[8,128,128]{2,1,0:T(8,128)(2,1)} custom-call(bf16[8,152,128]{2,1,0:T(8,128)(2,1)S(1)} %all-to-all-done.received, bf16[512,1024]{1,0:T(8,128)(2,1)S(1)} %inside.1.after.local), custom_call_target="tpu_custom_call" | custom-call | tf_op jit(solution)/shard_map/scan/pallas_call | solution.py:468
  30.4 0.0 copy-start.3
  30.4 3.7 %all-to-all-start.1 = ((bf16[8,128,128]{2,1,0:T(8,128)(2,1)}), bf16[8,128,128]{2,1,0:T(8,128)(2,1)S(1)}, u32[]{:S(2)}, u32[]{:S(2)}) async-start(bf16[8,128,128]{2,1,0:T(8,128)(2,1)} %scan.1.after), calls=%async_computation.1 | async-start | bytes 524288 | tf_op jit(solution)/shard_map/all_to_all | solution.py:474
  34.1 5.4 %gate.1 = (bf16[512,1024]{1,0:T(8,128)(2,1)S(1)}, f32[32,128]{1,0:T(8,128)S(1)}, f32[32,128]{1,0:T(8,128)S(1)}) custom-call(s32[1]{0:T(128)} %bitcast.rank, bf16[512,2048]{1,0:T(8,128)(2,1)} %states_hbm.3, bf16[2048,1024]{1,0:T(8,128)(2,1)} %gate_hbm.1, bf16[8,152,128]{2,1,0:T(8,128)(2,1)S(1)} %all-to-all-done.received, bf16[8,128,128]{2,1,0:T(8,128)(2,1)} %scan.1.after), custom_call_target="tpu_custom_call" | custom-call | flops 2147483648 | tf_op jit(solution)/shard_map/gate/pallas_call | solution.py:476
  39.4 3.1 %all-to-all-done.1 = bf16[8,128,128]{2,1,0:T(8,128)(2,1)S(1)} async-done(((bf16[8,128,128]{2,1,0:T(8,128)(2,1)}), bf16[8,128,128]{2,1,0:T(8,128)(2,1)S(1)}, u32[]{:S(2)}, u32[]{:S(2)}) %all-to-all-start.1) | async-done | bytes 262176 | tf_op jit(solution)/shard_map/all_to_all | solution.py:474
  42.5 0.0 copy-done.3
  42.5 0.0 copy-done.4
  42.5 1.0 %finish.1 = f32[32,8,128]{2,1,0:T(8,128)S(1)} custom-call(bf16[512,256]{1,0:T(8,128)(2,1)S(1)} %get-tuple-element.24.state, bf16[1024,128]{1,0:T(8,128)(2,1)S(1)} %bitcast.11, bf16[512,1024]{1,0:T(8,128)(2,1)S(1)} %inside.1.after.local, bf16[512,1024]{1,0:T(8,128)(2,1)S(1)} %get-tuple-element.27.gate, f32[512,128]{1,0:T(8,128)S(1)} %get-tuple-element.23.cols, ...), custom_call_target="tpu_custom_call" | custom-call | flops 157286400 | tf_op jit(solution)/shard_map/finish/pallas_call | solution.py:486
  43.6 11.5 %all_to_all.15.received = f32[32,8,128]{2,1,0:T(8,128)S(1)} all-to-all(f32[32,8,128]{2,1,0:T(8,128)S(1)} %finish.1), channel_id=1, replica_groups=mesh['seq'=8,'head'=4] {'seq','head'}, dimensions={0} | all-to-all | bytes 262144 | tf_op jit(solution)/shard_map/all_to_all | solution.py:501
  55.1 0.7 %loss.1 = (f32[4,128]{1,0:T(4,128)}, f32[4,128]{1,0:T(4,128)}, f32[1,1]{1,0:T(1,128)}) custom-call(s32[1]{0:T(128)} %bitcast.rank, f32[32,8,128]{2,1,0:T(8,128)S(1)} %all_to_all.15.received, f32[32,128]{1,0:T(8,128)S(1)} %get-tuple-element.28.returns, f32[32,128]{1,0:T(8,128)S(1)} %get-tuple-element.29.code), custom_call_target="tpu_custom_call" | custom-call | tf_op jit(solution)/shard_map/loss/pallas_call | solution.py:503
  (1 shorter events, 0.0 us)
Async XLA Ops:
  0.6 8.6 %copy-start = (bf16[2048,1024]{1,0:T(8,128)(2,1)S(1)}, bf16[2048,1024]{1,0:T(8,128)(2,1)}, u32[]{:S(2)}) copy-start(bf16[2048,1024]{1,0:T(8,128)(2,1)} %inner_w.3) | copy-start | bytes 12582916
  4.2 7.4 %copy-start.1 = (f32[4,1024]{1,0:T(4,128)S(1)}, f32[4,1024]{1,0:T(4,128)}, u32[]{:S(2)}) copy-start(f32[4,1024]{1,0:T(4,128)} %taps_inner.1) | copy-start | bytes 49156
  4.2 7.4 %copy-start.2 = (f32[4,256]{1,0:T(4,128)S(1)}, f32[4,256]{1,0:T(4,128)}, u32[]{:S(2)}) copy-start(f32[4,256]{1,0:T(4,128)} %taps_state.1) | copy-start | bytes 12292
  4.2 7.4 %copy-start.5 = (s32[512]{0:T(512)S(1)}, s32[512]{0:T(512)}, u32[]{:S(2)}) copy-start(s32[512]{0:T(512)} %param.28) | copy-start | bytes 6148
  4.2 7.4 %copy-start.6 = (f32[512]{0:T(512)S(1)}, f32[512]{0:T(512)}, u32[]{:S(2)}) copy-start(f32[512]{0:T(512)} %param.27) | copy-start | bytes 6148
  4.2 7.4 %copy-start.7 = (s32[512]{0:T(512)S(1)}, s32[512]{0:T(512)}, u32[]{:S(2)}) copy-start(s32[512]{0:T(512)} %param.29) | copy-start | bytes 6148
  4.2 7.4 %collective-permute-start = (bf16[8,2048]{1,0:T(8,128)(2,1)S(1)}, bf16[8,2048]{1,0:T(8,128)(2,1)S(1)}, u32[]{:S(2)}, u32[]{:S(2)}) collective-permute-start(bf16[8,2048]{1,0:T(8,128)(2,1)S(1)} %get-tuple-element.18), channel_id=1, source_target_pairs={{0,4},{4,8},{8,12},{12,16},{16,20},{20,24},{24,28},{1,5},{5,9},{9,... | collective-permute-start | bytes 98312 | tf_op jit(solution)/shard_map/ppermute | solution.py:426
  11.6 9.2 %copy-start.8 = (f32[8]{0:T(128)S(1)}, f32[8]{0:T(128)}, u32[]{:S(2)}) copy-start(f32[8]{0:T(128)} %skip.1) | copy-start | bytes 100
  15.0 14.7 %all-to-all-start = ((bf16[8,152,128]{2,1,0:T(8,128)(2,1)}), bf16[8,152,128]{2,1,0:T(8,128)(2,1)S(1)}, u32[]{:S(2)}, u32[]{:S(2)}) async-start(bf16[8,152,128]{2,1,0:T(8,128)(2,1)} %get-tuple-element.25), calls=%async_computation | async-start | bytes 622592 | tf_op jit(solution)/shard_map/all_to_all | solution.py:459
  30.4 12.2 %copy-start.3 = (f32[1024]{0:T(1024)S(1)}, f32[1024]{0:T(1024)}, u32[]{:S(2)}) copy-start(f32[1024]{0:T(1024)} %param.25) | copy-start | bytes 12292
  30.4 12.2 %copy-start.4 = (f32[1024]{0:T(1024)S(1)}, f32[1024]{0:T(1024)}, u32[]{:S(2)}) copy-start(f32[1024]{0:T(1024)} %param.26) | copy-start | bytes 12292
  30.4 12.2 %all-to-all-start.1 = ((bf16[8,128,128]{2,1,0:T(8,128)(2,1)}), bf16[8,128,128]{2,1,0:T(8,128)(2,1)S(1)}, u32[]{:S(2)}, u32[]{:S(2)}) async-start(bf16[8,128,128]{2,1,0:T(8,128)(2,1)} %scan.1.after), calls=%async_computation.1 | async-start | bytes 524288 | tf_op jit(solution)/shard_map/all_to_all | solution.py:474

commit v3 on v2

--- a/solution.py
+++ b/solution.py
@@ -14,6 +14,7 @@
 EPSILON = 1e-05
 LANES = 128
 HALO = 8
+CONV_ROWS = 32
 RESET = 300.0
 VMEM = pl.BlockSpec(memory_space=pltpu.VMEM)
 SMEM = pl.BlockSpec(memory_space=pltpu.SMEM)
@@ -56,44 +57,24 @@
     return out
 
 
-def entry_body(
-    bias_hbm,
-    decay_hbm,
-    done_hbm,
-    states_hbm,
-    state_hbm,
-    step_hbm,
-    states,
-    state_w,
-    state_pre,
-    rows,
-    cols,
-    edge,
-    step_w,
-    done,
-    bias,
-    decay,
-    arrived,
+def edge_body(states_hbm, edge, arrived):
+    rows = pl.ds(states_hbm.shape[0] - HALO, HALO)
+    copy = pltpu.make_async_copy(states_hbm.at[rows], edge, arrived)
+    copy.start()
+    copy.wait()
+
+
+def project_body(
+    bias, decay, done, states, step_w, state_w, inner_w, inner_pre, state_pre, rows, cols
 ):
     length = states.shape[0]
     heads = bias.shape[0]
-    pairs = [(states_hbm, states), (step_hbm, step_w), (done_hbm, done)]
-    pairs += [(bias_hbm, bias), (decay_hbm, decay), (state_hbm, state_w)]
-    copies = [pltpu.make_async_copy(*pair, arrived.at[i]) for i, pair in enumerate(pairs)]
-    for copy in copies:
-        copy.start()
-    for copy in copies:
-        copy.wait()
-    edge[...] = states[length - HALO :]
-    step_rows(bias, decay, done, states, step_w, rows, cols, heads, length)
     width = 2 * LANES
     for c in range(0, state_w.shape[1], width):
         state_pre[:, c : c + width] = dot(states[...], state_w[:, c : c + width]).astype(BF16)
-
-
-def project_body(states, inner_w, inner_pre):
-    width = 2 * LANES
     for c in range(0, inner_w.shape[1], width):
+        if c == width:
+            step_rows(bias, decay, done, states, step_w, rows, cols, heads, length)
         inner_pre[:, c : c + width] = dot(states[...], inner_w[:, c : c + width]).astype(BF16)
 
 
@@ -141,16 +122,17 @@
     heads = rows.shape[0] // 3
     shards = message.shape[0]
     depth = heads * LANES // shards
-    block = LANES
+    block = CONV_ROWS
 
     def convolve(rim, source, taps, target, c, scaled):
         slot = pad.at[c % 2]
         at = slice(c * LANES, (c + 1) * LANES)
         slot[0:HALO] = rim
-        slot[HALO:] = source[:, at].astype(F32)
         for r in range(0, length, block):
-            out = taps[0:1, at] * slot[r + HALO - 3 : r + HALO - 3 + block]
-            for k in range(1, 4):
+            here = source[r : r + block, at].astype(F32)
+            slot[r + HALO : r + HALO + block] = here
+            out = taps[3:4, at] * here
+            for k in range(3):
                 out = out + taps[k : k + 1, at] * slot[r + HALO - 3 + k : r + HALO - 3 + k + block]
             out = silu(out).astype(BF16)
             target[r : r + block, at] = out
@@ -394,43 +376,28 @@
     shape = jax.ShapeDtypeStruct
     done_row = done_flags.reshape(1, length)
 
-    states_near, state_weight, state_pre, rows, cols, edge = call(
-        entry_body,
+    edge = call(
+        edge_body,
+        shape((HALO, states.shape[1]), BF16),
+        [HBM],
+        [pltpu.SemaphoreType.DMA(())],
+        flops=2 * length * states.shape[1] * inner_width,
+        moved=4 * states.size,
+        name="edge",
+    )(in_hbm(states))
+    halo = lax.ppermute(edge, "seq", [(i, i + 1) for i in range(shards - 1)])
+    inner_pre, state_pre, rows, cols = call(
+        project_body,
         [
-            shape(states.shape, BF16),
-            shape(state_weight.shape, BF16),
+            shape((length, inner_width), BF16),
             shape((length, state_width), BF16),
             shape((3 * heads, length), F32),
             shape((length, LANES), F32),
-            shape((HALO, states.shape[1]), BF16),
         ],
-        [HBM] * 6,
-        [
-            pltpu.VMEM(step_weight.shape[::-1], BF16),
-            pltpu.VMEM((1, length), jnp.int32),
-            pltpu.SMEM((heads,), F32),
-            pltpu.SMEM((heads,), F32),
-            pltpu.SemaphoreType.DMA((6,)),
-        ],
-        flops=2 * length * states.shape[1] * inner_width,
-        moved=4 * states.size,
-        name="entry",
-    )(
-        in_hbm(step_bias),
-        in_hbm(decay_rate),
-        in_hbm(done_row),
-        in_hbm(states),
-        in_hbm(state_weight),
-        in_hbm(step_weight.T),
-    )
-    halo = lax.ppermute(edge, "seq", [(i, i + 1) for i in range(shards - 1)])
-    inner_pre = call(
-        project_body,
-        shape((length, inner_width), BF16),
-        [VMEM, VMEM],
-        flops=2 * length * states.shape[1] * inner_width,
+        [SMEM, SMEM] + [VMEM] * 5,
+        flops=2 * length * states.shape[1] * (inner_width + state_width),
         name="project",
-    )(states_near, inner_weight)
+    )(step_bias, decay_rate, done_row, states, step_weight.T, state_weight, inner_weight)
     inner, state, message = call(
         conv_body,
         [

time: 56.2 us -> 55.7 us (level)
  waiting for transfers between devices: 9.52 us -> 10.4 us
  starting transfers between devices: 14.5 us -> 13.7 us
  Pallas kernels: 19.4 us -> 18.6 us
    all_to_all x1, starting transfers between devices: 5.82 us -> 4.88 us  [per_device(): received = lax.all_to_all(message, 'seq', 0, 0, tiled=True)]
    pallas_call x2, Pallas kernels: 5.83 us -> 4.89 us  [the longest x1 3.98 us: per_device(): call(project_body, [shape((length, inner_width), BF16), shape((length, st...]
    all_to_all x1, waiting for transfers between devices: 6.43 us -> 7.27 us  [per_device(): received = lax.all_to_all(message, 'seq', 0, 0, tiled=True)]
  transfers between devices with their start and end apart: 3 -> 3, of which waited for: 2 -> 2; matrix products, arithmetic and copies ran while one was open for 0% -> 0% of each run, Pallas kernels for 18% -> 21%
where the time goes in v3:
time: 55.7 us; the launch traced here: 55.3 us
  Pallas kernels  18.6 us (33%)
  starting transfers between devices  13.7 us (25%)
  blocking collectives  11.6 us (21%)
  waiting for transfers between devices  10.4 us (19%)
  between operations  0.88 us (2%)
    all_to_all x1, blocking collectives, per_device(): everything = lax.all_to_all(parts, ('seq', 'head'), 0, 0, tiled=True)  11.6 us
    all_to_all x1, waiting for transfers between devices, per_device(): received = lax.all_to_all(message, 'seq', 0, 0, tiled=True)  7.27 us
    pallas_call x1, Pallas kernels, per_device(): call(gate_body, [shape((length, inner_width), BF16), trajectory, trajecto...  5.35 us
    ppermute x1, starting transfers between devices, per_device(): halo = lax.ppermute(edge, 'seq', [(i, i + 1) for i in range(shards - 1)])  5.14 us
    all_to_all x1, starting transfers between devices, per_device(): received = lax.all_to_all(message, 'seq', 0, 0, tiled=True)  4.88 us
    pallas_call x1, Pallas kernels, per_device(): call(project_body, [shape((length, inner_width), BF16), shape((length, st...  3.98 us
    all_to_all x1, starting transfers between devices, per_device(): lax.all_to_all(carried, 'seq', 0, 0, tiled=True)  3.73 us
    pallas_call x1, Pallas kernels, per_device(): call(conv_body, [shape((length, inner_width), BF16), shape((length, state...  3.44 us
  transfers between devices with their start and end apart: 3, of which 2 were waited for; matrix products, arithmetic and copies ran while one was open for 0% of the time, Pallas kernels for 21%

profile of v3, /device:TPU:0, one launch (start us, length us, event | category | flops | bytes accessed | tf_op | source)
XLA Modules:
  0.0 55.3 jit_solution(17122193596969836499)
XLA Ops:
  0.6 0.0 copy-start.9
  0.6 0.0 copy-start.6
  0.7 0.0 copy-start.10
  0.7 0.0 copy-start
  0.7 0.0 copy-start.1
  0.7 0.0 copy-start.11
  0.7 0.0 copy-start.12
  0.7 0.9 %edge.1 = bf16[8,2048]{1,0:T(8,128)(2,1)S(1)} custom-call(bf16[512,2048]{1,0:T(8,128)(2,1)} %states_hbm.3), custom_call_target="tpu_custom_call" | custom-call | flops 2147483648 | bytes 4194304 | tf_op jit(solution)/shard_map/edge/pallas_call | solution.py:379
  1.6 5.1 %collective-permute-start = (bf16[8,2048]{1,0:T(8,128)(2,1)S(1)}, bf16[8,2048]{1,0:T(8,128)(2,1)S(1)}, u32[]{:S(2)}, u32[]{:S(2)}) collective-permute-start(bf16[8,2048]{1,0:T(8,128)(2,1)S(1)} %edge.1), channel_id=1, source_target_pairs={{0,4},{4,8},{8,12},{12,16},{16,20},{20,24},{24,28},{1,5},{5,9},{9,... | collective-permute-start | bytes 98312 | tf_op jit(solution)/shard_map/ppermute | solution.py:388
  6.8 0.0 copy-done.9
  6.8 0.0 copy-done.6
  6.8 0.0 copy-done.10
  6.8 0.0 copy-done
  6.8 0.0 copy-start.2
  6.9 0.0 copy-start.3
  6.9 0.0 copy-start.7
  6.9 0.0 copy-start.8
  6.9 4.0 %project.1 = (bf16[512,1024]{1,0:T(8,128)(2,1)S(1)}, bf16[512,256]{1,0:T(8,128)(2,1)S(1)}, f32[24,512]{1,0:T(8,128)S(1)}, f32[512,128]{1,0:T(8,128)S(1)}) custom-call(f32[8]{0:T(128)S(1)} %copy-done.11, f32[8]{0:T(128)S(1)} %copy-done.12, s32[1,512]{1,0:T(1,128)S(1)} %bitcast.14, bf16[512,2048]{1,0:T(8,128)(2,1)S(1)} %copy-done.9, ...), custom_call_target="tpu_custom_call" | custom-call | flops 2684354560 | tf_op jit(solution)/shard_map/project/pallas_call | solution.py:389
  10.9 0.0 copy-start.13
  10.9 0.0 collective-permute-done.halo
  10.9 3.4 %conv.1 = (bf16[512,1024]{1,0:T(8,128)(2,1)S(1)}, bf16[512,256]{1,0:T(8,128)(2,1)S(1)}, bf16[8,152,128]{2,1,0:T(8,128)(2,1)}) custom-call(bf16[8,2048]{1,0:T(8,128)(2,1)S(1)} %collective-permute-done.halo, bf16[2048,1024]{1,0:T(8,128)(2,1)S(1)} %copy-done, bf16[2048,256]{1,0:T(8,128)(2,1)S(1)} %copy-done.1, ...), custom_call_target="tpu_custom_call" | custom-call | flops 314572800 | tf_op jit(solution)/shard_map/conv/pallas_call | solution.py:401
  14.4 4.9 %all-to-all-start = ((bf16[8,152,128]{2,1,0:T(8,128)(2,1)}), bf16[8,152,128]{2,1,0:T(8,128)(2,1)S(1)}, u32[]{:S(2)}, u32[]{:S(2)}) async-start(bf16[8,152,128]{2,1,0:T(8,128)(2,1)} %get-tuple-element.21), calls=%async_computation | async-start | bytes 622592 | tf_op jit(solution)/shard_map/all_to_all | solution.py:426
  19.3 2.4 %inside.1.after.local = bf16[512,1024]{1,0:T(8,128)(2,1)S(1)} custom-call(f32[8]{0:T(128)S(1)} %copy-done.13, bf16[512,1024]{1,0:T(8,128)(2,1)S(1)} %get-tuple-element.22.inner, bf16[512,256]{1,0:T(8,128)(2,1)S(1)} %get-tuple-element.20.state, f32[24,512]{1,0:T(8,128)S(1)} %get-tuple-element.18.rows, f32[512,128]{1,0:T(8,128)S(1)} %get-tuple-element.19.cols), custom_call_target="tpu_custom_call" | custom-call | flops 1073741824 | tf_op jit(solution)/shard_map/inside/pallas_call | solution.py:427
  21.7 7.3 %all-to-all-done.received = bf16[8,152,128]{2,1,0:T(8,128)(2,1)S(1)} async-done(((bf16[8,152,128]{2,1,0:T(8,128)(2,1)}), bf16[8,152,128]{2,1,0:T(8,128)(2,1)S(1)}, u32[]{:S(2)}, u32[]{:S(2)}) %all-to-all-start) | async-done | bytes 311328 | tf_op jit(solution)/shard_map/all_to_all | solution.py:426
  28.9 0.8 %scan.1.after = bf16[8,128,128]{2,1,0:T(8,128)(2,1)} custom-call(bf16[8,152,128]{2,1,0:T(8,128)(2,1)S(1)} %all-to-all-done.received, bf16[512,1024]{1,0:T(8,128)(2,1)S(1)} %inside.1.after.local), custom_call_target="tpu_custom_call" | custom-call | tf_op jit(solution)/shard_map/scan/pallas_call | solution.py:435
  29.7 3.7 %all-to-all-start.1 = ((bf16[8,128,128]{2,1,0:T(8,128)(2,1)}), bf16[8,128,128]{2,1,0:T(8,128)(2,1)S(1)}, u32[]{:S(2)}, u32[]{:S(2)}) async-start(bf16[8,128,128]{2,1,0:T(8,128)(2,1)} %scan.1.after), calls=%async_computation.1 | async-start | bytes 524288 | tf_op jit(solution)/shard_map/all_to_all | solution.py:441
  33.4 5.4 %gate.1 = (bf16[512,1024]{1,0:T(8,128)(2,1)S(1)}, f32[32,128]{1,0:T(8,128)S(1)}, f32[32,128]{1,0:T(8,128)S(1)}) custom-call(s32[1]{0:T(128)} %bitcast.rank, bf16[512,2048]{1,0:T(8,128)(2,1)} %states_hbm.3, bf16[2048,1024]{1,0:T(8,128)(2,1)} %gate_hbm.1, bf16[8,152,128]{2,1,0:T(8,128)(2,1)S(1)} %all-to-all-done.received, bf16[8,128,128]{2,1,0:T(8,128)(2,1)} %scan.1.after), custom_call_target="tpu_custom_call" | custom-call | flops 2147483648 | tf_op jit(solution)/shard_map/gate/pallas_call | solution.py:443
  38.8 3.2 %all-to-all-done.1 = bf16[8,128,128]{2,1,0:T(8,128)(2,1)S(1)} async-done(((bf16[8,128,128]{2,1,0:T(8,128)(2,1)}), bf16[8,128,128]{2,1,0:T(8,128)(2,1)S(1)}, u32[]{:S(2)}, u32[]{:S(2)}) %all-to-all-start.1) | async-done | bytes 262176 | tf_op jit(solution)/shard_map/all_to_all | solution.py:441
  42.0 0.0 copy-done.4
  42.0 1.0 %finish.1 = f32[32,8,128]{2,1,0:T(8,128)S(1)} custom-call(bf16[512,256]{1,0:T(8,128)(2,1)S(1)} %get-tuple-element.20.state, bf16[1024,128]{1,0:T(8,128)(2,1)S(1)} %bitcast.11, bf16[512,1024]{1,0:T(8,128)(2,1)S(1)} %inside.1.after.local, bf16[512,1024]{1,0:T(8,128)(2,1)S(1)} %get-tuple-element.23.gate, f32[512,128]{1,0:T(8,128)S(1)} %get-tuple-element.19.cols, ...), custom_call_target="tpu_custom_call" | custom-call | flops 157286400 | tf_op jit(solution)/shard_map/finish/pallas_call | solution.py:453
  43.0 11.6 %all_to_all.15.received = f32[32,8,128]{2,1,0:T(8,128)S(1)} all-to-all(f32[32,8,128]{2,1,0:T(8,128)S(1)} %finish.1), channel_id=1, replica_groups=mesh['seq'=8,'head'=4] {'seq','head'}, dimensions={0} | all-to-all | bytes 262144 | tf_op jit(solution)/shard_map/all_to_all | solution.py:468
  54.6 0.7 %loss.1 = (f32[4,128]{1,0:T(4,128)}, f32[4,128]{1,0:T(4,128)}, f32[1,1]{1,0:T(1,128)}) custom-call(s32[1]{0:T(128)} %bitcast.rank, f32[32,8,128]{2,1,0:T(8,128)S(1)} %all_to_all.15.received, f32[32,128]{1,0:T(8,128)S(1)} %get-tuple-element.24.returns, f32[32,128]{1,0:T(8,128)S(1)} %get-tuple-element.25.code), custom_call_target="tpu_custom_call" | custom-call | tf_op jit(solution)/shard_map/loss/pallas_call | solution.py:470
  (11 shorter events, 0.0 us)
Async XLA Ops:
  0.6 6.1 %copy-start.9 = (bf16[512,2048]{1,0:T(8,128)(2,1)S(1)}, bf16[512,2048]{1,0:T(8,128)(2,1)}, u32[]{:S(2)}) copy-start(bf16[512,2048]{1,0:T(8,128)(2,1)} %states_hbm.3) | copy-start | bytes 6291460
  0.6 6.1 %copy-start.6 = (s32[512]{0:T(512)S(1)}, s32[512]{0:T(512)}, u32[]{:S(2)}) copy-start(s32[512]{0:T(512)} %param.28) | copy-start | bytes 6148
  0.7 6.1 %copy-start.10 = (bf16[2048,8]{0,1:T(8,128)(2,1)S(1)}, bf16[2048,8]{0,1:T(8,128)(2,1)}, u32[]{:S(2)}) copy-start(bf16[2048,8]{0,1:T(8,128)(2,1)} %param.19) | copy-start | bytes 98308
  0.7 6.1 %copy-start = (bf16[2048,1024]{1,0:T(8,128)(2,1)S(1)}, bf16[2048,1024]{1,0:T(8,128)(2,1)}, u32[]{:S(2)}) copy-start(bf16[2048,1024]{1,0:T(8,128)(2,1)} %inner_w.3) | copy-start | bytes 12582916
  0.7 6.1 %copy-start.1 = (bf16[2048,256]{1,0:T(8,128)(2,1)S(1)}, bf16[2048,256]{1,0:T(8,128)(2,1)}, u32[]{:S(2)}) copy-start(bf16[2048,256]{1,0:T(8,128)(2,1)} %state_w.3) | copy-start | bytes 3145732
  0.7 6.1 %copy-start.11 = (f32[8]{0:T(128)S(1)}, f32[8]{0:T(128)}, u32[]{:S(2)}) copy-start(f32[8]{0:T(128)} %bias.1) | copy-start | bytes 100
  0.7 6.1 %copy-start.12 = (f32[8]{0:T(128)S(1)}, f32[8]{0:T(128)}, u32[]{:S(2)}) copy-start(f32[8]{0:T(128)} %decay.1) | copy-start | bytes 100
  1.6 9.3 %collective-permute-start = (bf16[8,2048]{1,0:T(8,128)(2,1)S(1)}, bf16[8,2048]{1,0:T(8,128)(2,1)S(1)}, u32[]{:S(2)}, u32[]{:S(2)}) collective-permute-start(bf16[8,2048]{1,0:T(8,128)(2,1)S(1)} %edge.1), channel_id=1, source_target_pairs={{0,4},{4,8},{8,12},{12,16},{16,20},{20,24},{24,28},{1,5},{5,9},{9,... | collective-permute-start | bytes 98312 | tf_op jit(solution)/shard_map/ppermute | solution.py:388
  6.8 4.1 %copy-start.2 = (f32[4,1024]{1,0:T(4,128)S(1)}, f32[4,1024]{1,0:T(4,128)}, u32[]{:S(2)}) copy-start(f32[4,1024]{1,0:T(4,128)} %taps_inner.1) | copy-start | bytes 49156
  6.9 4.1 %copy-start.3 = (f32[4,256]{1,0:T(4,128)S(1)}, f32[4,256]{1,0:T(4,128)}, u32[]{:S(2)}) copy-start(f32[4,256]{1,0:T(4,128)} %taps_state.1) | copy-start | bytes 12292
  6.9 4.1 %copy-start.7 = (f32[512]{0:T(512)S(1)}, f32[512]{0:T(512)}, u32[]{:S(2)}) copy-start(f32[512]{0:T(512)} %param.27) | copy-start | bytes 6148
  6.9 4.1 %copy-start.8 = (s32[512]{0:T(512)S(1)}, s32[512]{0:T(512)}, u32[]{:S(2)}) copy-start(s32[512]{0:T(512)} %param.29) | copy-start | bytes 6148
  10.9 8.4 %copy-start.13 = (f32[8]{0:T(128)S(1)}, f32[8]{0:T(128)}, u32[]{:S(2)}) copy-start(f32[8]{0:T(128)} %skip.1) | copy-start | bytes 100
  14.4 14.6 %all-to-all-start = ((bf16[8,152,128]{2,1,0:T(8,128)(2,1)}), bf16[8,152,128]{2,1,0:T(8,128)(2,1)S(1)}, u32[]{:S(2)}, u32[]{:S(2)}) async-start(bf16[8,152,128]{2,1,0:T(8,128)(2,1)} %get-tuple-element.21), calls=%async_computation | async-start | bytes 622592 | tf_op jit(solution)/shard_map/all_to_all | solution.py:426
  29.7 12.3 %copy-start.4 = (f32[1024]{0:T(1024)S(1)}, f32[1024]{0:T(1024)}, u32[]{:S(2)}) copy-start(f32[1024]{0:T(1024)} %param.25) | copy-start | bytes 12292
  29.7 12.3 %copy-start.5 = (f32[1024]{0:T(1024)S(1)}, f32[1024]{0:T(1024)}, u32[]{:S(2)}) copy-start(f32[1024]{0:T(1024)} %param.26) | copy-start | bytes 12292
  29.7 12.3 %all-to-all-start.1 = ((bf16[8,128,128]{2,1,0:T(8,128)(2,1)}), bf16[8,128,128]{2,1,0:T(8,128)(2,1)S(1)}, u32[]{:S(2)}, u32[]{:S(2)}) async-start(bf16[8,128,128]{2,1,0:T(8,128)(2,1)} %scan.1.after), calls=%async_computation.1 | async-start | bytes 524288 | tf_op jit(solution)/shard_map/all_to_all | solution.py:441

commit v4 on v3

--- a/solution.py
+++ b/solution.py
@@ -24,13 +24,14 @@
 BF16 = jnp.bfloat16
 
 
-def call(body, outs, ins, scratch=(), flops=0, moved=0, name=None, limit=10):
+def call(body, outs, ins, scratch=(), flops=0, moved=0, name=None, limit=10, alias=None):
     return pl.pallas_call(
         body,
         out_shape=outs,
         in_specs=ins,
         out_specs=jax.tree.map(lambda _: VMEM, outs),
         scratch_shapes=list(scratch),
+        input_output_aliases=alias or {},
         cost_estimate=pl.CostEstimate(flops=flops, transcendentals=0, bytes_accessed=moved),
         compiler_params=pltpu.CompilerParams(vmem_limit_bytes=limit * 2**20),
         name=name,
@@ -187,7 +188,10 @@
     gate_hbm,
     received,
     after,
-    gate,
+    local,
+    cols,
+    near,
+    far,
     returns,
     code,
     states,
@@ -207,9 +211,15 @@
     for copy in copies:
         copy.wait()
     width = 2 * LANES
+    heads = gate_w.shape[1] // LANES
     for c in range(0, gate_w.shape[1], width):
         pre = dot(states[...], gate_w[:, c : c + width]).astype(BF16).astype(F32)
-        gate[:, c : c + width] = silu(pre).astype(gate.dtype)
+        gate = silu(pre)
+        near[:, c : c + width] = (local[:, c : c + width].astype(F32) * gate).astype(BF16)
+        for half in range(0, width, LANES):
+            lane = 2 * heads + (c + half) // LANES
+            scaled = gate[:, half : half + LANES] * cols[:, lane : lane + 1]
+            far[:, c + half : c + half + LANES] = scaled.astype(BF16)
 
 
 def series(received, depth, per, returns, code, reward_s, alive_s, steps_s):
@@ -288,7 +298,7 @@
             local[r : r + block, at] = out.astype(local.dtype)
 
 
-def finish_body(state, carried, local, gate, cols, norm_gain, value_weight, message):
+def finish_body(state, carried, near, far, norm_gain, value_weight, message):
     length = state.shape[0]
     heads = carried.shape[0] // LANES
     block = LANES
@@ -306,9 +316,8 @@
             for i in range(2):
                 h = c + i
                 at = slice(h * LANES, (h + 1) * LANES)
-                reach = cols[r : r + block, 2 * heads + h : 2 * heads + h + 1]
-                mixed = local[r : r + block, at].astype(F32) + reach * fix[:, i * LANES : (i + 1) * LANES]
-                gated = mixed * gate[r : r + block, at].astype(F32)
+                fixed = far[r : r + block, at].astype(F32) * fix[:, i * LANES : (i + 1) * LANES]
+                gated = near[r : r + block, at].astype(F32) + fixed
                 square = square + gated * gated
                 total = total + gated * weight[:, at]
         squares.append(jnp.sum(square.T, axis=0, keepdims=True))
@@ -440,28 +449,29 @@
     )(received, local)
     entered = lax.all_to_all(carried, "seq", 0, 0, tiled=True).reshape(heads * LANES, LANES)
     trajectory = shape((shards * per, LANES), F32)
-    gate, returns, code = call(
+    wide = shape((length, inner_width), BF16)
+    near, far, returns, code = call(
         gate_body,
-        [shape((length, inner_width), BF16), trajectory, trajectory],
-        [SMEM, HBM, HBM, VMEM, ANY],
+        [wide, wide, trajectory, trajectory],
+        [SMEM, HBM, HBM, VMEM, ANY, VMEM, VMEM],
         [pltpu.VMEM(states.shape, BF16), pltpu.VMEM(gate_weight.shape, BF16)]
         + [pltpu.VMEM((shards * per, LANES), F32)] * 3
         + [pltpu.SemaphoreType.DMA((2,))],
         flops=2 * length * states.shape[1] * inner_width,
         name="gate",
-    )(rank, in_hbm(states), in_hbm(gate_weight), received, carried)
+        alias={5: 0},
+    )(rank, in_hbm(states), in_hbm(gate_weight), received, carried, local, cols)
     parts = call(
         finish_body,
         shape((devices, 2 * per, LANES), F32),
-        [VMEM] * 7,
+        [VMEM] * 6,
         flops=length * inner_width * 300,
         name="finish",
     )(
         state,
         entered,
-        local,
-        gate,
-        cols,
+        near,
+        far,
         norm_gain.reshape(1, inner_width),
         value_weight.reshape(1, inner_width),
     )

time: 55.7 us -> 55.5 us (level)
  waiting for transfers between devices: 10.4 us -> 9.14 us
  local copies, waits for them, and re-layouts: 0.07 us -> 1.02 us
    unnamed x28 -> x34, local copies, waits for them, and re-layouts: 0.07 us -> 1.02 us
    all_to_all x1, waiting for transfers between devices: 7.27 us -> 6.32 us  [per_device(): received = lax.all_to_all(message, 'seq', 0, 0, tiled=True)]
  transfers between devices with their start and end apart: 3 -> 3, of which waited for: 2 -> 2; matrix products, arithmetic and copies ran while one was open for 0% -> 0% of each run, Pallas kernels for 21% -> 22%
where the time goes in v4:
time: 55.5 us; the launch traced here: 55.1 us
  Pallas kernels  18.7 us (34%)
  starting transfers between devices  13.7 us (25%)
  blocking collectives  11.6 us (21%)
  waiting for transfers between devices  9.14 us (16%)
  local copies, waits for them, and re-layouts  1.02 us (2%)
  between operations  0.92 us (2%)
    all_to_all x1, blocking collectives, per_device(): everything = lax.all_to_all(parts, ('seq', 'head'), 0, 0, tiled=True)  11.6 us
    all_to_all x1, waiting for transfers between devices, per_device(): received = lax.all_to_all(message, 'seq', 0, 0, tiled=True)  6.32 us
    pallas_call x1, Pallas kernels, per_device(): call(gate_body, [wide, wide, trajectory, trajectory], [SMEM, HBM, HBM, VM...  5.68 us
    ppermute x1, starting transfers between devices, per_device(): halo = lax.ppermute(edge, 'seq', [(i, i + 1) for i in range(shards - 1)])  5.14 us
    all_to_all x1, starting transfers between devices, per_device(): received = lax.all_to_all(message, 'seq', 0, 0, tiled=True)  5.01 us
    pallas_call x1, Pallas kernels, per_device(): call(project_body, [shape((length, inner_width), BF16), shape((length, st...  3.98 us
    all_to_all x1, starting transfers between devices, per_device(): lax.all_to_all(carried, 'seq', 0, 0, tiled=True)  3.6 us
    pallas_call x1, Pallas kernels, per_device(): call(conv_body, [shape((length, inner_width), BF16), shape((length, state...  3.47 us
  transfers between devices with their start and end apart: 3, of which 2 were waited for; matrix products, arithmetic and copies ran while one was open for 0% of the time, Pallas kernels for 22%

profile of v4, /device:TPU:0, one launch (start us, length us, event | category | flops | bytes accessed | tf_op | source)
XLA Modules:
  0.0 55.1 jit_solution(16518313108054467098)
XLA Ops:
  0.6 0.0 copy-start.1
  0.6 0.0 copy-start.10
  0.7 0.0 copy-start.13
  0.7 0.0 copy-start
  0.7 0.0 copy-start.2
  0.7 0.0 copy-start.14
  0.7 0.0 copy-start.15
  0.7 0.9 %edge.1 = bf16[8,2048]{1,0:T(8,128)(2,1)S(1)} custom-call(bf16[512,2048]{1,0:T(8,128)(2,1)} %states_hbm.3), custom_call_target="tpu_custom_call" | custom-call | flops 2147483648 | bytes 4194304 | tf_op jit(solution)/shard_map/edge/pallas_call | solution.py:388
  1.6 5.1 %collective-permute-start = (bf16[8,2048]{1,0:T(8,128)(2,1)S(1)}, bf16[8,2048]{1,0:T(8,128)(2,1)S(1)}, u32[]{:S(2)}, u32[]{:S(2)}) collective-permute-start(bf16[8,2048]{1,0:T(8,128)(2,1)S(1)} %edge.1), channel_id=1, source_target_pairs={{0,4},{4,8},{8,12},{12,16},{16,20},{20,24},{24,28},{1,5},{5,9},{9,... | collective-permute-start | bytes 98312 | tf_op jit(solution)/shard_map/ppermute | solution.py:397
  6.8 0.0 copy-done.1
  6.8 0.0 copy-done.10
  6.8 0.0 copy-start.6
  6.9 0.0 copy-start.7
  6.9 0.0 copy-start.11
  6.9 0.0 copy-start.12
  6.9 4.0 %project.1 = (bf16[512,1024]{1,0:T(8,128)(2,1)S(1)}, bf16[512,256]{1,0:T(8,128)(2,1)S(1)}, f32[24,512]{1,0:T(8,128)S(1)}, f32[512,128]{1,0:T(8,128)S(1)}) custom-call(f32[8]{0:T(128)S(1)} %copy-done.14, f32[8]{0:T(128)S(1)} %copy-done.15, s32[1,512]{1,0:T(1,128)S(1)} %bitcast.14, bf16[512,2048]{1,0:T(8,128)(2,1)S(1)} %copy-done.1, ...), custom_call_target="tpu_custom_call" | custom-call | flops 2684354560 | tf_op jit(solution)/shard_map/project/pallas_call | solution.py:398
  10.9 0.0 copy-start.16
  10.9 0.0 collective-permute-done.halo
  10.9 3.5 %conv.1 = (bf16[512,1024]{1,0:T(8,128)(2,1)S(1)}, bf16[512,256]{1,0:T(8,128)(2,1)S(1)}, bf16[8,152,128]{2,1,0:T(8,128)(2,1)}) custom-call(bf16[8,2048]{1,0:T(8,128)(2,1)S(1)} %collective-permute-done.halo, bf16[2048,1024]{1,0:T(8,128)(2,1)S(1)} %copy-done, bf16[2048,256]{1,0:T(8,128)(2,1)S(1)} %copy-done.2, ...), custom_call_target="tpu_custom_call" | custom-call | flops 314572800 | tf_op jit(solution)/shard_map/conv/pallas_call | solution.py:410
  14.4 5.0 %all-to-all-start = ((bf16[8,152,128]{2,1,0:T(8,128)(2,1)}), bf16[8,152,128]{2,1,0:T(8,128)(2,1)S(1)}, u32[]{:S(2)}, u32[]{:S(2)}) async-start(bf16[8,152,128]{2,1,0:T(8,128)(2,1)} %get-tuple-element.22), calls=%async_computation | async-start | bytes 622592 | tf_op jit(solution)/shard_map/all_to_all | solution.py:435
  19.5 0.9 %copy-done.4 = f32[512,128]{1,0:T(8,128)S(1)} copy-done((f32[512,128]{1,0:T(8,128)S(1)}, f32[512,128]{1,0:T(8,128)}, u32[]{:S(2)}) %copy-start.4) | copy-done | bytes 262168
  20.4 2.4 %inside.1.after.local = bf16[512,1024]{1,0:T(8,128)(2,1)S(1)} custom-call(f32[8]{0:T(128)S(1)} %copy-done.16, bf16[512,1024]{1,0:T(8,128)(2,1)S(1)} %get-tuple-element.23.inner, bf16[512,256]{1,0:T(8,128)(2,1)S(1)} %get-tuple-element.21.state, f32[24,512]{1,0:T(8,128)S(1)} %get-tuple-element.19.rows, f32[512,128]{1,0:T(8,128)S(1)} %copy-done.4), custom_call_target="tpu_custom_call" | custom-call | flops 1073741824 | tf_op jit(solution)/shard_map/inside/pallas_call | solution.py:436
  22.8 6.3 %all-to-all-done.received = bf16[8,152,128]{2,1,0:T(8,128)(2,1)S(1)} async-done(((bf16[8,152,128]{2,1,0:T(8,128)(2,1)}), bf16[8,152,128]{2,1,0:T(8,128)(2,1)S(1)}, u32[]{:S(2)}, u32[]{:S(2)}) %all-to-all-start) | async-done | bytes 311328 | tf_op jit(solution)/shard_map/all_to_all | solution.py:435
  29.1 0.8 %scan.1.after = bf16[8,128,128]{2,1,0:T(8,128)(2,1)} custom-call(bf16[8,152,128]{2,1,0:T(8,128)(2,1)S(1)} %all-to-all-done.received, bf16[512,1024]{1,0:T(8,128)(2,1)S(1)} %inside.1.after.local), custom_call_target="tpu_custom_call" | custom-call | tf_op jit(solution)/shard_map/scan/pallas_call | solution.py:444
  29.9 3.6 %all-to-all-start.1 = ((bf16[8,128,128]{2,1,0:T(8,128)(2,1)}), bf16[8,128,128]{2,1,0:T(8,128)(2,1)S(1)}, u32[]{:S(2)}, u32[]{:S(2)}) async-start(bf16[8,128,128]{2,1,0:T(8,128)(2,1)} %scan.1.after), calls=%async_computation.1 | async-start | bytes 524288 | tf_op jit(solution)/shard_map/all_to_all | solution.py:450
  33.5 0.0 copy-start.9
  33.5 5.7 %gate.1 = (bf16[512,1024]{1,0:T(8,128)(2,1)S(1)}, bf16[512,1024]{1,0:T(8,128)(2,1)S(1)}, f32[32,128]{1,0:T(8,128)S(1)}, f32[32,128]{1,0:T(8,128)S(1)}) custom-call(s32[1]{0:T(128)} %bitcast.rank, bf16[512,2048]{1,0:T(8,128)(2,1)} %states_hbm.3, bf16[2048,1024]{1,0:T(8,128)(2,1)} %gate_hbm.1, ...), custom_call_target="tpu_custom_call", output_to_operand_aliasing={{0}: (5, {})} | custom-call | flops 2147483648 | tf_op jit(solution)/shard_map/gate/pallas_call | solution.py:453
  39.2 2.8 %all-to-all-done.1 = bf16[8,128,128]{2,1,0:T(8,128)(2,1)S(1)} async-done(((bf16[8,128,128]{2,1,0:T(8,128)(2,1)}), bf16[8,128,128]{2,1,0:T(8,128)(2,1)S(1)}, u32[]{:S(2)}, u32[]{:S(2)}) %all-to-all-start.1) | async-done | bytes 262176 | tf_op jit(solution)/shard_map/all_to_all | solution.py:450
  42.0 0.0 copy-done.9
  42.0 0.8 %finish.1 = f32[32,8,128]{2,1,0:T(8,128)S(1)} custom-call(bf16[512,256]{1,0:T(8,128)(2,1)S(1)} %get-tuple-element.21.state, bf16[1024,128]{1,0:T(8,128)(2,1)S(1)} %bitcast.11, bf16[512,1024]{1,0:T(8,128)(2,1)S(1)} %get-tuple-element.24.near, bf16[512,1024]{1,0:T(8,128)(2,1)S(1)} %get-tuple-element.25.far, f32[1,1024]{1,0:T(1,128)S(1)} %bitcast.12, ...), custom_call_target="tpu_custom_call" | custom-call | flops 157286400 | tf_op jit(solution)/shard_map/finish/pallas_call | solution.py:464
  42.8 11.6 %all_to_all.15.received = f32[32,8,128]{2,1,0:T(8,128)S(1)} all-to-all(f32[32,8,128]{2,1,0:T(8,128)S(1)} %finish.1), channel_id=1, replica_groups=mesh['seq'=8,'head'=4] {'seq','head'}, dimensions={0} | all-to-all | bytes 262144 | tf_op jit(solution)/shard_map/all_to_all | solution.py:478
  54.4 0.7 %loss.1 = (f32[4,128]{1,0:T(4,128)}, f32[4,128]{1,0:T(4,128)}, f32[1,1]{1,0:T(1,128)}) custom-call(s32[1]{0:T(128)} %bitcast.rank, f32[32,8,128]{2,1,0:T(8,128)S(1)} %all_to_all.15.received, f32[32,128]{1,0:T(8,128)S(1)} %get-tuple-element.26.returns, f32[32,128]{1,0:T(8,128)S(1)} %get-tuple-element.27.code), custom_call_target="tpu_custom_call" | custom-call | tf_op jit(solution)/shard_map/loss/pallas_call | solution.py:480
  (17 shorter events, 0.0 us)
Async XLA Ops:
  0.6 6.1 %copy-start.1 = (bf16[512,2048]{1,0:T(8,128)(2,1)S(1)}, bf16[512,2048]{1,0:T(8,128)(2,1)}, u32[]{:S(2)}) copy-start(bf16[512,2048]{1,0:T(8,128)(2,1)} %states_hbm.3) | copy-start | bytes 6291460
  0.6 6.1 %copy-start.10 = (s32[512]{0:T(512)S(1)}, s32[512]{0:T(512)}, u32[]{:S(2)}) copy-start(s32[512]{0:T(512)} %param.28) | copy-start | bytes 6148
  0.7 6.1 %copy-start.13 = (bf16[2048,8]{0,1:T(8,128)(2,1)S(1)}, bf16[2048,8]{0,1:T(8,128)(2,1)}, u32[]{:S(2)}) copy-start(bf16[2048,8]{0,1:T(8,128)(2,1)} %param.19) | copy-start | bytes 98308
  0.7 6.1 %copy-start = (bf16[2048,1024]{1,0:T(8,128)(2,1)S(1)}, bf16[2048,1024]{1,0:T(8,128)(2,1)}, u32[]{:S(2)}) copy-start(bf16[2048,1024]{1,0:T(8,128)(2,1)} %inner_w.3) | copy-start | bytes 12582916
  0.7 6.1 %copy-start.2 = (bf16[2048,256]{1,0:T(8,128)(2,1)S(1)}, bf16[2048,256]{1,0:T(8,128)(2,1)}, u32[]{:S(2)}) copy-start(bf16[2048,256]{1,0:T(8,128)(2,1)} %state_w.3) | copy-start | bytes 3145732
  0.7 6.1 %copy-start.14 = (f32[8]{0:T(128)S(1)}, f32[8]{0:T(128)}, u32[]{:S(2)}) copy-start(f32[8]{0:T(128)} %bias.1) | copy-start | bytes 100
  0.7 6.1 %copy-start.15 = (f32[8]{0:T(128)S(1)}, f32[8]{0:T(128)}, u32[]{:S(2)}) copy-start(f32[8]{0:T(128)} %decay.1) | copy-start | bytes 100
  1.6 9.3 %collective-permute-start = (bf16[8,2048]{1,0:T(8,128)(2,1)S(1)}, bf16[8,2048]{1,0:T(8,128)(2,1)S(1)}, u32[]{:S(2)}, u32[]{:S(2)}) collective-permute-start(bf16[8,2048]{1,0:T(8,128)(2,1)S(1)} %edge.1), channel_id=1, source_target_pairs={{0,4},{4,8},{8,12},{12,16},{16,20},{20,24},{24,28},{1,5},{5,9},{9,... | collective-permute-start | bytes 98312 | tf_op jit(solution)/shard_map/ppermute | solution.py:397
  6.8 4.1 %copy-start.6 = (f32[4,1024]{1,0:T(4,128)S(1)}, f32[4,1024]{1,0:T(4,128)}, u32[]{:S(2)}) copy-start(f32[4,1024]{1,0:T(4,128)} %taps_inner.1) | copy-start | bytes 49156
  6.9 4.1 %copy-start.7 = (f32[4,256]{1,0:T(4,128)S(1)}, f32[4,256]{1,0:T(4,128)}, u32[]{:S(2)}) copy-start(f32[4,256]{1,0:T(4,128)} %taps_state.1) | copy-start | bytes 12292
  6.9 4.1 %copy-start.11 = (f32[512]{0:T(512)S(1)}, f32[512]{0:T(512)}, u32[]{:S(2)}) copy-start(f32[512]{0:T(512)} %param.27) | copy-start | bytes 6148
  6.9 4.1 %copy-start.12 = (s32[512]{0:T(512)S(1)}, s32[512]{0:T(512)}, u32[]{:S(2)}) copy-start(s32[512]{0:T(512)} %param.29) | copy-start | bytes 6148
  10.9 3.5 %copy-start.3 = (f32[512,128]{1,0:T(8,128)}, f32[512,128]{1,0:T(8,128)S(1)}, u32[]{:S(2)}) copy-start(f32[512,128]{1,0:T(8,128)S(1)} %get-tuple-element.20.cols) | copy-start | bytes 786436
  10.9 8.6 %copy-start.16 = (f32[8]{0:T(128)S(1)}, f32[8]{0:T(128)}, u32[]{:S(2)}) copy-start(f32[8]{0:T(128)} %skip.1) | copy-start | bytes 100
  14.4 19.1 %copy-start.5 = (f32[512,128]{1,0:T(8,128)S(1)}, f32[512,128]{1,0:T(8,128)}, u32[]{:S(2)}) copy-start(f32[512,128]{1,0:T(8,128)} %copy-done.3) | copy-start | bytes 786436
  14.4 14.7 %all-to-all-start = ((bf16[8,152,128]{2,1,0:T(8,128)(2,1)}), bf16[8,152,128]{2,1,0:T(8,128)(2,1)S(1)}, u32[]{:S(2)}, u32[]{:S(2)}) async-start(bf16[8,152,128]{2,1,0:T(8,128)(2,1)} %get-tuple-element.22), calls=%async_computation | async-start | bytes 622592 | tf_op jit(solution)/shard_map/all_to_all | solution.py:435
  19.4 1.0 %copy-start.4 = (f32[512,128]{1,0:T(8,128)S(1)}, f32[512,128]{1,0:T(8,128)}, u32[]{:S(2)}) copy-start(f32[512,128]{1,0:T(8,128)} %copy-done.3) | copy-start | bytes 786436
  29.9 12.1 %all-to-all-start.1 = ((bf16[8,128,128]{2,1,0:T(8,128)(2,1)}), bf16[8,128,128]{2,1,0:T(8,128)(2,1)S(1)}, u32[]{:S(2)}, u32[]{:S(2)}) async-start(bf16[8,128,128]{2,1,0:T(8,128)(2,1)} %scan.1.after), calls=%async_computation.1 | async-start | bytes 524288 | tf_op jit(solution)/shard_map/all_to_all | solution.py:450
  33.5 8.5 %copy-start.8 = (f32[1024]{0:T(1024)S(1)}, f32[1024]{0:T(1024)}, u32[]{:S(2)}) copy-start(f32[1024]{0:T(1024)} %param.25) | copy-start | bytes 12292
  33.5 8.5 %copy-start.9 = (f32[1024]{0:T(1024)S(1)}, f32[1024]{0:T(1024)}, u32[]{:S(2)}) copy-start(f32[1024]{0:T(1024)} %param.26) | copy-start | bytes 12292
